TPU v7x, 128 devices: a whole 4x4x4 slice. The times are simulated.
128 devices in a mesh: row: 32 (over x, y, core), col: 4 (over z).
Axes of the slice: x: 4, y: 4, z: 4, core: 2. Of those that a mesh axis runs over, the one named last changes fastest.
Arguments:
- eigvecs: float32 [8192, 4096], P('row', 'col'), may hold values from -6 to 6
- reflectors: float32 [32, 32, 64, 192], P('row'), may hold values from -0.5 to 1.5, as said below
- factors: float32 [32, 32, 64, 64], P('row'), may hold values from -3 to 3, as said below
- first_block: int32 [32], replicated, may hold values from 0 to 31
- live_count: int32 [4], P('col'), may hold values from 128 to 768
Outputs:
- vectors: float32 [8192, 4096], P('row', 'col')
Inputs may be any that keep to these rules, and one draw needn't show every extreme that they name: reflectors[w, g, j, 0] lies in 1 to 1.5; the other entries are small. factors[w, g] is upper triangular, and I - V_wg factors[w, g] V_wg^T equals the product over j = 0 .. 63 in order of I - 2 v_j v_j^T / (v_j^T v_j), v_j the columns of V_wg.
All inputs are finite; a program needn't handle non-finite values.
Results may differ from a plain program's by a relative error of at most 0.0003.
Values sent between devices are 32-bit elements; how exact they have to be, the bound alone decides.
A program may use at most 64 MiB of HBM per device.

v0:
```python
import jax
import jax.numpy as jnp
from jax import lax
from jax.sharding import PartitionSpec as P

highest_precision = lax.Precision.HIGHEST


def sent_together(arrays, axis, split_dim, concat_dim, along):
    both = jnp.concatenate(arrays, axis=along)
    filled, at, gathered = (
        lax.all_to_all(both, axis, split_axis=split_dim, concat_axis=concat_dim, tiled=True),
        0,
        [],
    )
    for a in arrays:
        gathered.append(lax.slice_in_dim(filled, at, at + a.shape[along], axis=along))
        at += a.shape[along]
    return tuple(gathered)


def passed_along(x, axis, by):
    count = lax.axis_size(axis)
    pairs = [(i, i + by) for i in range(count) if 0 <= i + by < count]
    return lax.ppermute(x, axis, pairs)


def expand(compact):
    block_width, band_width = compact.shape
    block_rows = block_width + band_width
    padded = jnp.pad(compact, ((0, 0), (0, block_rows + 1 - band_width)))
    flattened = padded.reshape(block_width * (block_rows + 1))[: block_width * block_rows]
    return flattened.reshape(block_width, block_rows).T


def apply_one(z_block, compact, factor):
    expanded_factor = expand(compact)
    correlation_matrix = lax.dot_general(
        expanded_factor,
        z_block,
        (((0,), (0,)), ((), ())),
        precision=highest_precision,
        preferred_element_type=jnp.float32,
    )
    correlation_matrix = jnp.dot(
        factor, correlation_matrix, precision=highest_precision, preferred_element_type=jnp.float32
    )
    return z_block - jnp.dot(
        expanded_factor,
        correlation_matrix,
        precision=highest_precision,
        preferred_element_type=jnp.float32,
    )


def unchanged(z_block, compact, factor):
    return z_block


def sweep_block_list(eigenvector_blocks, compact_forms, factor_collection, active_window):

    def advance_sweep(carry, element):
        z_block, compact, factor, flag = element
        return (carry, lax.cond(flag, apply_one, unchanged, z_block, compact, factor))

    unused_slot, final_result = lax.scan(
        advance_sweep, 0, (eigenvector_blocks, compact_forms, factor_collection, active_window)
    )
    return final_result


def body(eigvecs, reflectors, factors, first_block, live_count):
    row_devices = lax.axis_size("row")
    position = lax.axis_index("row")
    row_count, col_count = eigvecs.shape
    window_share, total_blocks, block_width, band_width = reflectors.shape
    block_rows = block_width + band_width
    half_block = block_rows // 2
    per_device = row_count // block_rows
    compact_all, factor_all = sent_together((reflectors, factors), "row", 1, 0, 3)
    window_count = compact_all.shape[0]
    first_row_block = position * per_device
    local_index = jnp.arange(per_device, dtype=jnp.int32) + first_row_block

    def window_pair(number, vectors):
        even_window = 2 * number
        odd_window = even_window + 1
        compact = compact_all[even_window]
        factor = factor_all[even_window]
        active_window = local_index >= first_block[even_window]
        blocks = vectors.reshape(per_device, block_rows, col_count)
        vectors = sweep_block_list(blocks, compact, factor, active_window).reshape(
            row_count, col_count
        )
        compact = compact_all[odd_window]
        factor = factor_all[odd_window]
        active_window = local_index >= first_block[odd_window]
        interior = vectors[half_block : row_count - half_block].reshape(
            per_device - 1, block_rows, col_count
        )
        interior = sweep_block_list(
            interior,
            compact[: per_device - 1],
            factor[: per_device - 1],
            active_window[: per_device - 1],
        )
        interior = interior.reshape(row_count - block_rows, col_count)
        straddle_on = active_window[per_device - 1] & (position < row_devices - 1)
        from_below = passed_along(vectors[:half_block], "row", -1)
        from_above, above_compact, above_factor = passed_along(
            (vectors[row_count - half_block :], compact[per_device - 1], factor[per_device - 1]),
            "row",
            1,
        )
        joined = jnp.concatenate([vectors[row_count - half_block :], from_below], axis=0)
        bottom_part = lax.cond(
            straddle_on,
            apply_one,
            unchanged,
            joined,
            compact[per_device - 1],
            factor[per_device - 1],
        )[:half_block]
        upper_on = (position > 0) & (first_row_block - 1 >= first_block[odd_window])
        joined_upper = jnp.concatenate([from_above, vectors[:half_block]], axis=0)
        top_part = lax.cond(
            upper_on, apply_one, unchanged, joined_upper, above_compact, above_factor
        )[half_block:]
        return jnp.concatenate([top_part, interior, bottom_part], axis=0)

    vectors = lax.fori_loop(0, window_count // 2, window_pair, eigvecs)
    slot_index = jnp.arange(col_count, dtype=jnp.int32)
    kept_mask = slot_index < live_count[0]
    return jnp.where(kept_mask[None, :], vectors, jnp.zeros_like(vectors))


def solution(mesh):
    placed = (
        P("row", "col"),
        P("row", None, None, None),
        P("row", None, None, None),
        P(),
        P("col"),
    )
    return jax.shard_map(
        body, mesh=mesh, in_specs=placed, out_specs=P("row", "col"), check_vma=False
    )
```

profile of v0, /device:TPU:6, one launch (start us, length us, event | category | flops | bytes accessed | tf_op | source)
XLA Modules:
  0.0 519.1 jit_solution(5617881592009704229)
XLA Ops:
  4.6 7.6 %all-to-all-start = ((f32[1,32,64,256]{3,2,0,1:T(8,128)}), f32[1,32,64,256]{3,2,0,1:T(8,128)S(1)}, u32[]{:S(2)}, u32[]{:S(2)}) async-start(f32[1,32,64,256]{3,2,0,1:T(8,128)} %pad_maximum_fusion.3), calls=%async_computation | async-start | bytes 4194304 | tf_op jit(solution)/shard_map/all_to_all | solution.py:12
  12.9 25.7 %all-to-all-done = f32[1,32,64,256]{3,2,0,1:T(8,128)S(1)} async-done(((f32[1,32,64,256]{3,2,0,1:T(8,128)}), f32[1,32,64,256]{3,2,0,1:T(8,128)S(1)}, u32[]{:S(2)}, u32[]{:S(2)}) %all-to-all-start) | async-done | bytes 2097184 | tf_op jit(solution)/shard_map/all_to_all | solution.py:12
  41.4 476.6 %while.24 = (s32[]{:T(128)}, f32[256,1024]{1,0:T(8,128)S(1)}, s32[32]{0:T(128)S(1)}, s32[]{:T(128)}, pred[]{:T(512)}, /*index=5*/s32[1]{0:T(128)}, f32[32,1,64,1...) while((s32[]{:T(128)}, f32[256,1024]{1,0:T(8,128)S(1)}, ...), condition=%wide.region_7.8_spmd, body=%wide.region_0.7_spmd.sunk | while | flops 1360527360 | bytes 33934720 | solution.py:131
  42.6 4.8 conditional.6
  64.1 4.8 conditional.7
  74.4 4.8 conditional.6
  97.3 4.8 conditional.7
  135.2 4.8 conditional.6
  160.5 4.8 conditional.6
  182.5 4.8 conditional.7
  192.8 4.8 conditional.6
  225.2 4.8 conditional.6
  303.6 4.8 conditional.7
  313.9 4.8 conditional.6
  345.6 5.7 %collective-permute-start = (f32[128,1024]{1,0:T(8,128)S(1)}, f32[128,1024]{1,0:T(8,128)S(1)}, u32[]{:S(2)}, u32[]{:S(2)}) collective-permute-start(f32[128,1024]{1,0:T(8,128)S(1)} %get-tuple-element.459), channel_id=1, source_target_pairs={{4,0},{8,4},{12,8},{16,12},{20,16},{24,20},{28,24},{32,28},{36,32}... | collective-permute-start | bytes 1572872 | tf_op jit(solution)/shard_map/while/body/eval_jaxpr/ppermute | solution.py:25
  368.5 4.8 conditional.6
  385.6 5.0 collective-permute-start.3
  393.2 4.8 conditional.7
  421.3 4.8 conditional.7
  431.7 4.8 conditional.6
  436.7 5.7 %collective-permute-start = (f32[128,1024]{1,0:T(8,128)S(1)}, f32[128,1024]{1,0:T(8,128)S(1)}, u32[]{:S(2)}, u32[]{:S(2)}) collective-permute-start(f32[128,1024]{1,0:T(8,128)S(1)} %get-tuple-element.459), channel_id=1, source_target_pairs={{4,0},{8,4},{12,8},{16,12},{20,16},{24,20},{28,24},{32,28},{36,32}... | collective-permute-start | bytes 1572872 | tf_op jit(solution)/shard_map/while/body/eval_jaxpr/ppermute | solution.py:25
  459.4 4.8 conditional.6
  481.4 4.8 conditional.7
  508.9 4.8 conditional.7
  (636 shorter events, 499.2 us)
Async XLA Ops:
  4.6 34.0 %all-to-all-start = ((f32[1,32,64,256]{3,2,0,1:T(8,128)}), f32[1,32,64,256]{3,2,0,1:T(8,128)S(1)}, u32[]{:S(2)}, u32[]{:S(2)}) async-start(f32[1,32,64,256]{3,2,0,1:T(8,128)} %pad_maximum_fusion.3), calls=%async_computation | async-start | bytes 4194304 | tf_op jit(solution)/shard_map/all_to_all | solution.py:12
  53.7 16.0 %collective-permute-start.2 = (f32[64,192]{1,0:T(8,128)}, f32[64,192]{1,0:T(8,128)S(1)}, u32[]{:S(2)}, u32[]{:S(2)}) collective-permute-start(f32[64,192]{1,0:T(8,128)} %dynamic-slice_bitcast_fusion.5), channel_id=1, source_target_pairs={{0,4},{4,8},{8,12},{12,16},{16,20},{20,24},{24,28},{28,32},{32,36}... | collective-permute-start | bytes 147464 | tf_op jit(solution)/shard_map/while/body/eval_jaxpr/ppermute | solution.py:25
  79.4 14.2 %collective-permute-start = (f32[128,1024]{1,0:T(8,128)S(1)}, f32[128,1024]{1,0:T(8,128)S(1)}, u32[]{:S(2)}, u32[]{:S(2)}) collective-permute-start(f32[128,1024]{1,0:T(8,128)S(1)} %get-tuple-element.459), channel_id=1, source_target_pairs={{4,0},{8,4},{12,8},{16,12},{20,16},{24,20},{28,24},{32,28},{36,32}... | collective-permute-start | bytes 1572872 | tf_op jit(solution)/shard_map/while/body/eval_jaxpr/ppermute | solution.py:25
  87.0 16.0 %collective-permute-start.2 = (f32[64,192]{1,0:T(8,128)}, f32[64,192]{1,0:T(8,128)S(1)}, u32[]{:S(2)}, u32[]{:S(2)}) collective-permute-start(f32[64,192]{1,0:T(8,128)} %dynamic-slice_bitcast_fusion.5), channel_id=1, source_target_pairs={{0,4},{4,8},{8,12},{12,16},{16,20},{20,24},{24,28},{28,32},{32,36}... | collective-permute-start | bytes 147464 | tf_op jit(solution)/shard_map/while/body/eval_jaxpr/ppermute | solution.py:25
  114.5 16.0 %collective-permute-start.2 = (f32[64,192]{1,0:T(8,128)}, f32[64,192]{1,0:T(8,128)S(1)}, u32[]{:S(2)}, u32[]{:S(2)}) collective-permute-start(f32[64,192]{1,0:T(8,128)} %dynamic-slice_bitcast_fusion.5), channel_id=1, source_target_pairs={{0,4},{4,8},{8,12},{12,16},{16,20},{20,24},{24,28},{28,32},{32,36}... | collective-permute-start | bytes 147464 | tf_op jit(solution)/shard_map/while/body/eval_jaxpr/ppermute | solution.py:25
  172.1 16.0 %collective-permute-start.2 = (f32[64,192]{1,0:T(8,128)}, f32[64,192]{1,0:T(8,128)S(1)}, u32[]{:S(2)}, u32[]{:S(2)}) collective-permute-start(f32[64,192]{1,0:T(8,128)} %dynamic-slice_bitcast_fusion.5), channel_id=1, source_target_pairs={{0,4},{4,8},{8,12},{12,16},{16,20},{20,24},{24,28},{28,32},{32,36}... | collective-permute-start | bytes 147464 | tf_op jit(solution)/shard_map/while/body/eval_jaxpr/ppermute | solution.py:25
  197.8 15.0 %collective-permute-start = (f32[128,1024]{1,0:T(8,128)S(1)}, f32[128,1024]{1,0:T(8,128)S(1)}, u32[]{:S(2)}, u32[]{:S(2)}) collective-permute-start(f32[128,1024]{1,0:T(8,128)S(1)} %get-tuple-element.459), channel_id=1, source_target_pairs={{4,0},{8,4},{12,8},{16,12},{20,16},{24,20},{28,24},{32,28},{36,32}... | collective-permute-start | bytes 1572872 | tf_op jit(solution)/shard_map/while/body/eval_jaxpr/ppermute | solution.py:25
  204.5 16.0 %collective-permute-start.2 = (f32[64,192]{1,0:T(8,128)}, f32[64,192]{1,0:T(8,128)S(1)}, u32[]{:S(2)}, u32[]{:S(2)}) collective-permute-start(f32[64,192]{1,0:T(8,128)} %dynamic-slice_bitcast_fusion.5), channel_id=1, source_target_pairs={{0,4},{4,8},{8,12},{12,16},{16,20},{20,24},{24,28},{28,32},{32,36}... | collective-permute-start | bytes 147464 | tf_op jit(solution)/shard_map/while/body/eval_jaxpr/ppermute | solution.py:25
  230.2 14.6 %collective-permute-start = (f32[128,1024]{1,0:T(8,128)S(1)}, f32[128,1024]{1,0:T(8,128)S(1)}, u32[]{:S(2)}, u32[]{:S(2)}) collective-permute-start(f32[128,1024]{1,0:T(8,128)S(1)} %get-tuple-element.459), channel_id=1, source_target_pairs={{4,0},{8,4},{12,8},{16,12},{20,16},{24,20},{28,24},{32,28},{36,32}... | collective-permute-start | bytes 1572872 | tf_op jit(solution)/shard_map/while/body/eval_jaxpr/ppermute | solution.py:25
  236.8 16.0 %collective-permute-start.2 = (f32[64,192]{1,0:T(8,128)}, f32[64,192]{1,0:T(8,128)S(1)}, u32[]{:S(2)}, u32[]{:S(2)}) collective-permute-start(f32[64,192]{1,0:T(8,128)} %dynamic-slice_bitcast_fusion.5), channel_id=1, source_target_pairs={{0,4},{4,8},{8,12},{12,16},{16,20},{20,24},{24,28},{28,32},{32,36}... | collective-permute-start | bytes 147464 | tf_op jit(solution)/shard_map/while/body/eval_jaxpr/ppermute | solution.py:25
  257.7 14.6 %collective-permute-start = (f32[128,1024]{1,0:T(8,128)S(1)}, f32[128,1024]{1,0:T(8,128)S(1)}, u32[]{:S(2)}, u32[]{:S(2)}) collective-permute-start(f32[128,1024]{1,0:T(8,128)S(1)} %get-tuple-element.459), channel_id=1, source_target_pairs={{4,0},{8,4},{12,8},{16,12},{20,16},{24,20},{28,24},{32,28},{36,32}... | collective-permute-start | bytes 1572872 | tf_op jit(solution)/shard_map/while/body/eval_jaxpr/ppermute | solution.py:25
  265.7 16.0 %collective-permute-start.2 = (f32[64,192]{1,0:T(8,128)}, f32[64,192]{1,0:T(8,128)S(1)}, u32[]{:S(2)}, u32[]{:S(2)}) collective-permute-start(f32[64,192]{1,0:T(8,128)} %dynamic-slice_bitcast_fusion.5), channel_id=1, source_target_pairs={{0,4},{4,8},{8,12},{12,16},{16,20},{20,24},{24,28},{28,32},{32,36}... | collective-permute-start | bytes 147464 | tf_op jit(solution)/shard_map/while/body/eval_jaxpr/ppermute | solution.py:25
  293.2 16.0 %collective-permute-start.2 = (f32[64,192]{1,0:T(8,128)}, f32[64,192]{1,0:T(8,128)S(1)}, u32[]{:S(2)}, u32[]{:S(2)}) collective-permute-start(f32[64,192]{1,0:T(8,128)} %dynamic-slice_bitcast_fusion.5), channel_id=1, source_target_pairs={{0,4},{4,8},{8,12},{12,16},{16,20},{20,24},{24,28},{28,32},{32,36}... | collective-permute-start | bytes 147464 | tf_op jit(solution)/shard_map/while/body/eval_jaxpr/ppermute | solution.py:25
  318.9 14.9 %collective-permute-start = (f32[128,1024]{1,0:T(8,128)S(1)}, f32[128,1024]{1,0:T(8,128)S(1)}, u32[]{:S(2)}, u32[]{:S(2)}) collective-permute-start(f32[128,1024]{1,0:T(8,128)S(1)} %get-tuple-element.459), channel_id=1, source_target_pairs={{4,0},{8,4},{12,8},{16,12},{20,16},{24,20},{28,24},{32,28},{36,32}... | collective-permute-start | bytes 1572872 | tf_op jit(solution)/shard_map/while/body/eval_jaxpr/ppermute | solution.py:25
  325.5 15.3 %collective-permute-start.2 = (f32[64,192]{1,0:T(8,128)}, f32[64,192]{1,0:T(8,128)S(1)}, u32[]{:S(2)}, u32[]{:S(2)}) collective-permute-start(f32[64,192]{1,0:T(8,128)} %dynamic-slice_bitcast_fusion.5), channel_id=1, source_target_pairs={{0,4},{4,8},{8,12},{12,16},{16,20},{20,24},{24,28},{28,32},{32,36}... | collective-permute-start | bytes 147464 | tf_op jit(solution)/shard_map/while/body/eval_jaxpr/ppermute | solution.py:25
  345.6 18.5 %collective-permute-start = (f32[128,1024]{1,0:T(8,128)S(1)}, f32[128,1024]{1,0:T(8,128)S(1)}, u32[]{:S(2)}, u32[]{:S(2)}) collective-permute-start(f32[128,1024]{1,0:T(8,128)S(1)} %get-tuple-element.459), channel_id=1, source_target_pairs={{4,0},{8,4},{12,8},{16,12},{20,16},{24,20},{28,24},{32,28},{36,32}... | collective-permute-start | bytes 1572872 | tf_op jit(solution)/shard_map/while/body/eval_jaxpr/ppermute | solution.py:25
  373.5 18.4 %collective-permute-start = (f32[128,1024]{1,0:T(8,128)S(1)}, f32[128,1024]{1,0:T(8,128)S(1)}, u32[]{:S(2)}, u32[]{:S(2)}) collective-permute-start(f32[128,1024]{1,0:T(8,128)S(1)} %get-tuple-element.459), channel_id=1, source_target_pairs={{4,0},{8,4},{12,8},{16,12},{20,16},{24,20},{28,24},{32,28},{36,32}... | collective-permute-start | bytes 1572872 | tf_op jit(solution)/shard_map/while/body/eval_jaxpr/ppermute | solution.py:25
  376.6 15.5 %collective-permute-start.1 = (f32[128,1024]{1,0:T(8,128)S(1)}, f32[128,1024]{1,0:T(8,128)S(1)}, u32[]{:S(2)}, u32[]{:S(2)}) collective-permute-start(f32[128,1024]{1,0:T(8,128)S(1)} %get-tuple-element.460), channel_id=1, source_target_pairs={{0,4},{4,8},{8,12},{12,16},{16,20},{20,24},{24,28},{28,32},{32,36}... | collective-permute-start | bytes 1572872 | tf_op jit(solution)/shard_map/while/body/eval_jaxpr/ppermute | solution.py:25
  380.6 18.4 %collective-permute-start.2 = (f32[64,192]{1,0:T(8,128)}, f32[64,192]{1,0:T(8,128)S(1)}, u32[]{:S(2)}, u32[]{:S(2)}) collective-permute-start(f32[64,192]{1,0:T(8,128)} %dynamic-slice_bitcast_fusion.5), channel_id=1, source_target_pairs={{0,4},{4,8},{8,12},{12,16},{16,20},{20,24},{24,28},{28,32},{32,36}... | collective-permute-start | bytes 147464 | tf_op jit(solution)/shard_map/while/body/eval_jaxpr/ppermute | solution.py:25
  403.7 16.3 %collective-permute-start = (f32[128,1024]{1,0:T(8,128)S(1)}, f32[128,1024]{1,0:T(8,128)S(1)}, u32[]{:S(2)}, u32[]{:S(2)}) collective-permute-start(f32[128,1024]{1,0:T(8,128)S(1)} %get-tuple-element.459), channel_id=1, source_target_pairs={{4,0},{8,4},{12,8},{16,12},{20,16},{24,20},{28,24},{32,28},{36,32}... | collective-permute-start | bytes 1572872 | tf_op jit(solution)/shard_map/while/body/eval_jaxpr/ppermute | solution.py:25
  411.7 15.3 %collective-permute-start.2 = (f32[64,192]{1,0:T(8,128)}, f32[64,192]{1,0:T(8,128)S(1)}, u32[]{:S(2)}, u32[]{:S(2)}) collective-permute-start(f32[64,192]{1,0:T(8,128)} %dynamic-slice_bitcast_fusion.5), channel_id=1, source_target_pairs={{0,4},{4,8},{8,12},{12,16},{16,20},{20,24},{24,28},{28,32},{32,36}... | collective-permute-start | bytes 147464 | tf_op jit(solution)/shard_map/while/body/eval_jaxpr/ppermute | solution.py:25
  436.7 15.7 %collective-permute-start = (f32[128,1024]{1,0:T(8,128)S(1)}, f32[128,1024]{1,0:T(8,128)S(1)}, u32[]{:S(2)}, u32[]{:S(2)}) collective-permute-start(f32[128,1024]{1,0:T(8,128)S(1)} %get-tuple-element.459), channel_id=1, source_target_pairs={{4,0},{8,4},{12,8},{16,12},{20,16},{24,20},{28,24},{32,28},{36,32}... | collective-permute-start | bytes 1572872 | tf_op jit(solution)/shard_map/while/body/eval_jaxpr/ppermute | solution.py:25
  471.1 16.0 %collective-permute-start.2 = (f32[64,192]{1,0:T(8,128)}, f32[64,192]{1,0:T(8,128)S(1)}, u32[]{:S(2)}, u32[]{:S(2)}) collective-permute-start(f32[64,192]{1,0:T(8,128)} %dynamic-slice_bitcast_fusion.5), channel_id=1, source_target_pairs={{0,4},{4,8},{8,12},{12,16},{16,20},{20,24},{24,28},{28,32},{32,36}... | collective-permute-start | bytes 147464 | tf_op jit(solution)/shard_map/while/body/eval_jaxpr/ppermute | solution.py:25
  498.6 16.0 %collective-permute-start.2 = (f32[64,192]{1,0:T(8,128)}, f32[64,192]{1,0:T(8,128)S(1)}, u32[]{:S(2)}, u32[]{:S(2)}) collective-permute-start(f32[64,192]{1,0:T(8,128)} %dynamic-slice_bitcast_fusion.5), channel_id=1, source_target_pairs={{0,4},{4,8},{8,12},{12,16},{16,20},{20,24},{24,28},{28,32},{32,36}... | collective-permute-start | bytes 147464 | tf_op jit(solution)/shard_map/while/body/eval_jaxpr/ppermute | solution.py:25
  (76 other events, 788.6 us)
where the time goes:
time: 527 us; the launch traced here: 519 us
  starting transfers between devices  175 us (33%)
  matrix products  124 us (24%)
  local copies, waits for them, and re-layouts  107 us (20%)
  waiting for transfers between devices  51.8 us (10%)
  loops' own time  35.8 us (7%)
  other arithmetic  25.2 us (5%)
    ppermute x64, starting transfers between devices, passed_along(): return lax.ppermute(x, axis, pairs)  167 us
    dot_general x36, matrix products, apply_one(): jnp.dot(factor, correlation_matrix, precision=highest_precision, preferre...  53.5 us
    dot_general x36, matrix products, apply_one(): jnp.dot(expanded_factor, correlation_matrix, precision=highest_precision,...  43.1 us
    another operation x1, loops' own time, body(): vectors = lax.fori_loop(0, window_count // 2, window_pair, eigvecs)  33.9 us
    dot_general x36, matrix products, apply_one(): lax.dot_general(expanded_factor, z_block, (((0,), (0,)), ((), ())), preci...  27.1 us
    ppermute x64, waiting for transfers between devices, passed_along(): return lax.ppermute(x, axis, pairs)  26.1 us
    all_to_all x1, waiting for transfers between devices, sent_together(): lax.all_to_all(both, axis, split_axis=split_dim, concat_axis=concat_dim,...  25.7 us
    squeeze x16, local copies, waits for them, and re-layouts, window_pair(): compact[per_device - 1]  23.5 us
  transfers between devices with their start and end apart: 65, of which 13 were waited for; matrix products, arithmetic and copies ran while one was open for 27% of the time, Pallas kernels for 0%

commit v1 on v0

v1 whole, which is shorter than its diff:
```python
import functools

import jax
import jax.numpy as jnp
from jax import lax
from jax.experimental import pallas as pl
from jax.experimental.pallas import tpu as pltpu
from jax.sharding import PartitionSpec as P

HIGHEST = lax.Precision.HIGHEST
MAX_LIVE = 768
CHUNK = 256
AHEAD = 3
F32 = jnp.float32
BF16 = jnp.bfloat16


def split(x):
    hi = x.astype(BF16)
    lo = (x - hi.astype(F32)).astype(BF16)
    return hi, lo


def dot(a, b):
    return jnp.dot(a, b, preferred_element_type=F32)


def dot_full(a, b, dims=(((1,), (0,)), ((), ()))):
    return lax.dot_general(a, b, dims, precision=HIGHEST, preferred_element_type=F32)


TN = (((0,), (0,)), ((), ()))


def kernel(
    n_row,
    eig_ref,
    refl_ref,
    out_ref,
    y_ref,
    g_ref,
    cs_ref,
    cr_ref,
    fw_ref,
    rh_ref,
    rl_ref,
    sh_ref,
    sl_ref,
    hs_ref,
    hl_ref,
    w_ref,
    ws_ref,
    wl_ref,
    send_sem,
    recv_sem,
    fsend_sem,
    frecv_sem,
):
    d = lax.axis_index("row")
    has_up = d > 0
    has_dn = d < n_row - 1
    windows, nb, block_rows = refl_ref.shape
    rounds = windows // 2
    half = block_rows // 2
    band = block_rows - nb
    n_chunks = y_ref.shape[0]

    def link(way, p, c):
        src = cs_ref.at[p, c, pl.ds(way * nb, nb)]
        dst = cr_ref.at[p, c, pl.ds((1 - way) * nb, nb)]
        return pltpu.make_async_remote_copy(
            src_ref=src,
            dst_ref=dst,
            send_sem=send_sem.at[way, p, c],
            recv_sem=recv_sem.at[way, p, c],
            device_id={"row": d + 2 * way - 1},
            device_id_type=pl.DeviceIdType.MESH,
        )

    def forward(r):
        return pltpu.make_async_remote_copy(
            src_ref=refl_ref.at[2 * r + 1],
            dst_ref=fw_ref.at[r],
            send_sem=fsend_sem.at[r],
            recv_sem=frecv_sem.at[r],
            device_id={"row": d + 1},
            device_id_type=pl.DeviceIdType.MESH,
        )

    barrier = pltpu.get_barrier_semaphore()

    @pl.when(has_up)
    def _():
        pl.semaphore_signal(
            barrier, inc=1, device_id={"row": d - 1}, device_id_type=pl.DeviceIdType.MESH
        )

    @pl.when(has_dn)
    def _():
        pl.semaphore_signal(
            barrier, inc=1, device_id={"row": d + 1}, device_id_type=pl.DeviceIdType.MESH
        )

    inside = has_up & has_dn

    @pl.when(inside)
    def _():
        pl.semaphore_wait(barrier, 2)

    @pl.when(jnp.logical_not(inside))
    def _():
        pl.semaphore_wait(barrier, 1)

    @pl.when(has_dn)
    def _():
        for r in range(min(AHEAD, rounds)):
            forward(r).start()

    @pl.when(jnp.logical_not(has_up))
    def _():
        fw_ref[...] = jnp.zeros_like(fw_ref)
        for p in range(2):
            for c in range(n_chunks):
                cr_ref[p, c, pl.ds(0, nb)] = jnp.zeros((nb, CHUNK), F32)

    @pl.when(jnp.logical_not(has_dn))
    def _():
        for p in range(2):
            for c in range(n_chunks):
                cr_ref[p, c, pl.ds(nb, nb)] = jnp.zeros((nb, CHUNK), F32)

    def expanded(block):
        lane = lax.broadcasted_iota(jnp.int32, (nb, block_rows), 1)
        return pltpu.roll(jnp.where(lane < band, block, 0.0), 0, 1, stride=1, stride_axis=0)

    lane_h = lax.broadcasted_iota(jnp.int32, (nb, half), 1)

    def prepare_even(r):
        block = refl_ref[2 * r]
        vt = expanded(block)
        factor = jnp.where(lane_h >= half - nb, block[:, half:], 0.0)
        u = dot_full(factor, jnp.concatenate([vt, vt], axis=0))
        op = dot_full(vt, u, TN)
        hi, lo = split(op)
        rh_ref[...] = hi
        rl_ref[...] = lo
        return op

    def prepare_odd(r, op):
        q = lax.rem(r, 2)
        own = refl_ref[2 * r + 1]
        other = fw_ref[r]
        none = jnp.zeros((nb, half), F32)
        proj = jnp.concatenate(
            [
                jnp.concatenate([expanded(other)[:, half:], none], axis=1),
                jnp.concatenate([none, expanded(own)[:, :half]], axis=1),
            ],
            axis=0,
        )
        both = jnp.concatenate(
            [
                jnp.where(lane_h < nb, pltpu.roll(other[:, half:], nb, 1), 0.0),
                jnp.where(lane_h >= half - nb, own[:, half:], 0.0),
            ],
            axis=0,
        )
        w = dot_full(proj, both, TN)
        w_ref[q] = w
        whi, wlo = split(w)
        ws_ref[q] = jnp.concatenate([whi, whi], axis=1)
        wl_ref[q] = wlo
        s = proj - dot_full(proj, op)
        shi, slo = split(s)
        sh_ref[...] = shi
        sl_ref[...] = slo
        return s

    def prepare_link(r, s):
        h = dot_full(s, w_ref[1 - lax.rem(r, 2)])
        hhi, hlo = split(h)
        hs_ref[...] = jnp.concatenate([hhi, hhi], axis=1)
        hl_ref[...] = hlo

    def arrive(r):
        @pl.when(has_up)
        def _():
            forward(r).wait_recv()

    def launch(p, c):
        @pl.when(has_up)
        def _():
            link(0, p, c).start()

        @pl.when(has_dn)
        def _():
            link(1, p, c).start()

    def land(p, c):
        @pl.when(has_up)
        def _():
            link(0, p, c).wait_send()
            link(1, p, c).wait_recv()

        @pl.when(has_dn)
        def _():
            link(1, p, c).wait_send()
            link(0, p, c).wait_recv()

    def project(y):
        yh, yl = split(y)
        return dot(sh_ref[...], yh) + (dot(sl_ref[...], yh) + dot(sh_ref[...], yl))

    def reflect(z):
        zh, zl = split(z)
        return z - (dot(rh_ref[...], zh) + (dot(rl_ref[...], zh) + dot(rh_ref[...], zl)))

    def columns(c):
        return pl.ds(c * CHUNK, CHUNK)

    op = prepare_even(0)
    arrive(0)
    prepare_odd(0, op)
    for c in range(n_chunks):
        cs_ref[0, c] = project(eig_ref[:, columns(c)])
        launch(0, c)
    for c in range(n_chunks):
        y_ref[c] = reflect(eig_ref[:, columns(c)])

    def next_round(r):
        op = prepare_even(r)
        arrive(r)
        s = prepare_odd(r, op)
        prepare_link(r, s)
        for c in range(n_chunks):
            g_ref[c] = project(y_ref[c])

    next_round(1)

    def step(r, carry):
        p = lax.rem(r, 2)

        @pl.when(has_dn & (r + AHEAD < rounds))
        def _():
            forward(r + AHEAD).start()

        for c in range(n_chunks):
            land(p, c)
            total = cs_ref[p, c] + cr_ref[p, c]
            thi, tlo = split(total)
            stacked = jnp.concatenate([thi, tlo], axis=0)
            cs_ref[1 - p, c] = g_ref[c] - (dot(hs_ref[...], stacked) + dot(hl_ref[...], thi))
            launch(1 - p, c)
            z = y_ref[c] - (dot(ws_ref[p], stacked) + dot(wl_ref[p], thi))
            y_ref[c] = reflect(z)

        @pl.when(r + 2 < rounds)
        def _():
            next_round(r + 2)

        return carry

    lax.fori_loop(0, rounds - 1, step, 0)

    p = (rounds - 1) % 2
    for c in range(n_chunks):
        land(p, c)
        total = cs_ref[p, c] + cr_ref[p, c]
        thi, tlo = split(total)
        stacked = jnp.concatenate([thi, tlo], axis=0)
        out_ref[:, columns(c)] = y_ref[c] - (dot(ws_ref[p], stacked) + dot(wl_ref[p], thi))

    @pl.when(has_dn)
    def _():
        def done(r, carry):
            forward(r).wait_send()
            return carry

        lax.fori_loop(0, rounds, done, 0)


def sweep(eigvecs, packed, n_row):
    rows = eigvecs.shape[0]
    windows, nb, block_rows = packed.shape
    rounds = windows // 2
    n_chunks = MAX_LIVE // CHUNK
    vmem = pltpu.VMEM
    return pl.pallas_call(
        functools.partial(kernel, n_row),
        out_shape=jax.ShapeDtypeStruct((rows, MAX_LIVE), F32),
        grid=(1,),
        in_specs=[
            pl.BlockSpec((rows, MAX_LIVE), lambda i: (0, 0)),
            pl.BlockSpec((windows, nb, block_rows), lambda i: (0, 0, 0)),
        ],
        out_specs=pl.BlockSpec((rows, MAX_LIVE), lambda i: (0, 0)),
        scratch_shapes=[
            vmem((n_chunks, rows, CHUNK), F32),
            vmem((n_chunks, 2 * nb, CHUNK), F32),
            vmem((2, n_chunks, 2 * nb, CHUNK), F32),
            vmem((2, n_chunks, 2 * nb, CHUNK), F32),
            vmem((rounds, nb, block_rows), F32),
            vmem((rows, rows), BF16),
            vmem((rows, rows), BF16),
            vmem((2 * nb, rows), BF16),
            vmem((2 * nb, rows), BF16),
            vmem((2 * nb, 4 * nb), BF16),
            vmem((2 * nb, 2 * nb), BF16),
            vmem((2, rows, 2 * nb), F32),
            vmem((2, rows, 4 * nb), BF16),
            vmem((2, rows, 2 * nb), BF16),
            pltpu.SemaphoreType.DMA((2, 2, n_chunks)),
            pltpu.SemaphoreType.DMA((2, 2, n_chunks)),
            pltpu.SemaphoreType.DMA((rounds,)),
            pltpu.SemaphoreType.DMA((rounds,)),
        ],
        compiler_params=pltpu.CompilerParams(
            collective_id=0, has_side_effects=True, vmem_limit_bytes=48 * 2**20
        ),
        name="sweep",
    )(eigvecs, packed)


def body(eigvecs, reflectors, factors, first_block, live_count):
    n_row = lax.axis_size("row")
    position = lax.axis_index("row")
    share, blocks = reflectors.shape[:2]
    window = position * share + jnp.arange(share, dtype=jnp.int32)
    block = jnp.arange(blocks, dtype=jnp.int32)
    applied = block[None, :] >= first_block[window][:, None]
    applied &= (window[:, None] % 2 == 0) | (block[None, :] < blocks - 1)
    factors = jnp.where(applied[:, :, None, None], factors, 0.0)
    packed = jnp.concatenate([reflectors, factors], axis=3)
    packed = lax.all_to_all(packed, "row", split_axis=1, concat_axis=0, tiled=True)
    packed = packed.reshape((packed.shape[0],) + packed.shape[2:])
    vectors = sweep(eigvecs, packed, n_row)
    col_count = eigvecs.shape[1]
    vectors = jnp.pad(vectors, ((0, 0), (0, col_count - MAX_LIVE)))
    kept_mask = jnp.arange(col_count, dtype=jnp.int32) < live_count[0]
    return jnp.where(kept_mask[None, :], vectors, 0.0)


def solution(mesh):
    placed = (
        P("row", "col"),
        P("row", None, None, None),
        P("row", None, None, None),
        P(),
        P("col"),
    )
    return jax.shard_map(
        body, mesh=mesh, in_specs=placed, out_specs=P("row", "col"), check_vma=False
    )
```

time: 527 us -> 118 us (0.22); the launches traced: 519 us -> 118 us
  starting transfers between devices: 175 us -> 7.74 us
  matrix products: 124 us -> 0 us
  local copies, waits for them, and re-layouts: 107 us -> 1.4 us
  Pallas kernels: 0 us -> 77.3 us
  loops' own time: 35.8 us -> 0 us
  waiting for transfers between devices: 51.8 us -> 25.7 us
  other arithmetic: 25.2 us -> 4.82 us
    ppermute x64 -> x0, starting transfers between devices: 167 us -> none  [passed_along(): return lax.ppermute(x, axis, pairs)]
    dot_general x108 -> x0, matrix products: 124 us -> none  [the longest x36 53.5 us: apply_one(): jnp.dot(factor, correlation_matrix, precision=highest_precision, preferre...]
    pallas_call x0 -> x1, Pallas kernels: none -> 77.3 us  [sweep(): pl.pallas_call(functools.partial(kernel, n_row), out_shape=jax.ShapeDtype...]
    squeeze x42 -> x0, local copies, waits for them, and re-layouts: 53.8 us -> none  [the longest x16 23.5 us: window_pair(): compact[per_device - 1]]
    another operation x49 -> x0, loops' own time: 35.8 us -> none  [the longest x1 33.9 us: body(): vectors = lax.fori_loop(0, window_count // 2, window_pair, eigvecs)]
    ppermute x64 -> x0, waiting for transfers between devices: 26.1 us -> none  [passed_along(): return lax.ppermute(x, axis, pairs)]
    concatenate x49 -> x1, other arithmetic: 24.2 us -> 1.73 us  [body(): packed = jnp.concatenate([reflectors, factors], axis=3)]
    slice x84 -> x0, local copies, waits for them, and re-layouts: 15.9 us -> none  [the longest x16 13.3 us: window_pair(): lax.cond(straddle_on, apply_one, unchanged, joined, compact[per_device -...]
  transfers between devices with their start and end apart: 65 -> 1, of which waited for: 13 -> 1; matrix products, arithmetic and copies ran while one was open for 27% -> 0% of each run, Pallas kernels for 0% -> 0%
where the time goes in v1:
time: 118 us
  Pallas kernels  77.3 us (66%)
  waiting for transfers between devices  25.7 us (22%)
  starting transfers between devices  7.74 us (7%)
  other arithmetic  4.82 us (4%)
  local copies, waits for them, and re-layouts  1.4 us (1%)
    pallas_call x1, Pallas kernels, sweep(): pl.pallas_call(functools.partial(kernel, n_row), out_shape=jax.ShapeDtype...  77.3 us
    all_to_all x1, waiting for transfers between devices, body(): lax.all_to_all(packed, 'row', split_axis=1, concat_axis=0, tiled=True)  25.7 us
    all_to_all x1, starting transfers between devices, body(): lax.all_to_all(packed, 'row', split_axis=1, concat_axis=0, tiled=True)  7.74 us
  transfers between devices with their start and end apart: 1, of which 1 were waited for; matrix products, arithmetic and copies ran while one was open for 0% of the time, Pallas kernels for 0%

profile of v1, /device:TPU:6, one launch (start us, length us, event | category | flops | bytes accessed | tf_op | source)
XLA Modules:
  0.0 117.6 jit_solution(15297306037386960613)
XLA Ops:
  0.0 0.0 copy-start.1
  0.0 1.4 %dynamic-slice.2 = s32[1]{0:T(128)} dynamic-slice(s32[32]{0:T(128)} %param.8, s32[]{:T(128)} %bitcast.3), dynamic_slice_sizes={1} | dynamic-slice | bytes 12 | tf_op jit(solution)/shard_map/gather | solution.py:330
  1.4 0.6 or_and_fusion
  2.0 1.4 %bitcast_select_fusion = f32[1,32,64,64]{3,2,0,1:T(8,128)S(1)} fusion(f32[1,32,64,64]{3,2,1,0:T(8,128)} %param.7, pred[32]{0:T(512)(128)(4,1)S(1)} %or_and_fusion), kind=kLoop, calls=%fused_computation.1 | loop fusion | flops 131072 | bytes 1048608 | tf_op jit(solution)/shard_map/jit(_where)/select_n | solution.py:332
  3.4 0.0 copy-done.1
  3.4 1.7 %pad_maximum_fusion = f32[1,32,64,256]{3,2,0,1:T(8,128)} fusion(f32[1,32,64,64]{3,2,0,1:T(8,128)S(1)} %bitcast_select_fusion, f32[1,32,64,192]{3,2,0,1:T(8,128)S(1)} %bitcast.12), kind=kLoop, calls=%fused_computation | loop fusion | flops 524288 | bytes 4194304 | tf_op jit(solution)/shard_map/concatenate | solution.py:333
  5.1 0.0 copy-start
  5.1 7.7 %all-to-all-start = ((f32[1,32,64,256]{3,2,0,1:T(8,128)}), f32[1,32,64,256]{3,2,0,1:T(8,128)S(1)}, u32[]{:S(2)}, u32[]{:S(2)}) async-start(f32[1,32,64,256]{3,2,0,1:T(8,128)} %pad_maximum_fusion), calls=%async_computation | async-start | bytes 4194304 | tf_op jit(solution)/shard_map/all_to_all | solution.py:334
  13.5 25.7 %all-to-all-done = f32[1,32,64,256]{3,2,0,1:T(8,128)S(1)} async-done(((f32[1,32,64,256]{3,2,0,1:T(8,128)}), f32[1,32,64,256]{3,2,0,1:T(8,128)S(1)}, u32[]{:S(2)}, u32[]{:S(2)}) %all-to-all-start) | async-done | bytes 2097184 | tf_op jit(solution)/shard_map/all_to_all | solution.py:334
  39.2 0.0 copy-done
  39.2 77.3 %sweep.1 = f32[256,768]{1,0:T(8,128)S(1)} custom-call(f32[256,1024]{1,0:T(8,128)S(1)} %copy-done, f32[32,64,256]{2,1,0:T(8,128)S(1)} %bitcast.11), custom_call_target="tpu_custom_call" | custom-call | tf_op jit(solution)/shard_map/sweep/pallas_call | solution.py:288
  116.5 1.1 pad_select_fusion
  (1 shorter events, 0.0 us)
Async XLA Ops:
  0.0 3.4 %copy-start.1 = (f32[1,32,64,192]{3,2,1,0:T(8,128)S(1)}, f32[1,32,64,192]{3,2,1,0:T(8,128)}, u32[]{:S(2)}) copy-start(f32[1,32,64,192]{3,2,1,0:T(8,128)} %param.6) | copy-start | bytes 4718596
  5.1 34.1 %copy-start = (f32[256,1024]{1,0:T(8,128)S(1)}, f32[256,1024]{1,0:T(8,128)}, u32[]{:S(2)}) copy-start(f32[256,1024]{1,0:T(8,128)} %eig_ref.1) | copy-start | bytes 3145732
  5.1 34.1 %all-to-all-start = ((f32[1,32,64,256]{3,2,0,1:T(8,128)}), f32[1,32,64,256]{3,2,0,1:T(8,128)S(1)}, u32[]{:S(2)}, u32[]{:S(2)}) async-start(f32[1,32,64,256]{3,2,0,1:T(8,128)} %pad_maximum_fusion), calls=%async_computation | async-start | bytes 4194304 | tf_op jit(solution)/shard_map/all_to_all | solution.py:334

commit v2 on v1

v2 whole, which is shorter than its diff:
```python
import functools

import jax
import jax.numpy as jnp
from jax import lax
from jax.experimental import pallas as pl
from jax.experimental.pallas import tpu as pltpu
from jax.sharding import PartitionSpec as P

MAX_LIVE = 768
CHUNK = 256
AHEAD = 3
LEAD = 12
F32 = jnp.float32
BF16 = jnp.bfloat16
MESH = pl.DeviceIdType.MESH
TN = (((0,), (0,)), ((), ()))


def split(x):
    hi = x.astype(BF16)
    lo = (x - hi.astype(F32)).astype(BF16)
    return hi, lo


def dot(a, b):
    return jnp.dot(a, b, preferred_element_type=F32)


def dot_tn(a, b):
    return lax.dot_general(a, b, TN, preferred_element_type=F32)


def kernel(
    n_row,
    n_col,
    first_ref,
    eig_hbm,
    refl_hbm,
    fact_hbm,
    out_ref,
    e_ref,
    v_ref,
    t_ref,
    pk_ref,
    got_ref,
    fw_ref,
    y_ref,
    g_ref,
    st_ref,
    cs_ref,
    cr_ref,
    rh_ref,
    rl_ref,
    sh_ref,
    sl_ref,
    hs_ref,
    hl_ref,
    ws_ref,
    wl_ref,
    local_sem,
    eig_sem,
    asend_sem,
    rsend_sem,
    arecv_sem,
    send_sem,
    recv_sem,
    fsend_sem,
    frecv_sem,
):
    d = lax.axis_index("row")
    z = lax.axis_index("col")
    has_up = d > 0
    has_dn = d < n_row - 1
    windows, nb, block_rows = got_ref.shape
    band = block_rows - nb
    rounds = windows // 2
    half = block_rows // 2
    n_chunks = y_ref.shape[0]
    n_peers = n_row // n_col
    kin = lax.rem(z - d + n_row * n_col, n_col)

    def peer(j):
        return kin + n_col * j

    barrier = pltpu.get_barrier_semaphore()

    def greet(cond, where):
        @pl.when(cond)
        def _():
            pl.semaphore_signal(barrier, inc=1, device_id=where, device_id_type=MESH)

    for j in range(n_peers):
        greet(peer(j) != d, {"row": peer(j)})
    for o in range(1, n_col):
        pl.semaphore_signal(
            barrier, inc=1, device_id={"col": lax.rem(z + o, n_col)}, device_id_type=MESH
        )
    greet(has_up, {"row": d - 1})
    greet(has_dn, {"row": d + 1})

    def fetch(j):
        t = peer(j) if j < n_peers else d
        return (
            pltpu.make_async_copy(refl_hbm.at[0, t], v_ref.at[j], local_sem.at[0, j]),
            pltpu.make_async_copy(fact_hbm.at[0, t], t_ref.at[j], local_sem.at[1, j]),
        )

    for j in range(n_peers + 1):
        for copy in fetch(j):
            copy.start()
    eig_copy = pltpu.make_async_copy(
        eig_hbm.at[:, pl.ds(0, n_chunks * CHUNK)], e_ref, eig_sem
    )
    eig_copy.start()

    @pl.when(jnp.logical_not(has_up))
    def _():
        fw_ref[...] = jnp.zeros_like(fw_ref)
        for p in range(2):
            for c in range(n_chunks):
                cr_ref[p, c, pl.ds(0, nb)] = jnp.zeros((nb, CHUNK), F32)

    @pl.when(jnp.logical_not(has_dn))
    def _():
        for p in range(2):
            for c in range(n_chunks):
                cr_ref[p, c, pl.ds(nb, nb)] = jnp.zeros((nb, CHUNK), F32)

    for j in range(n_peers + 1):
        for copy in fetch(j):
            copy.wait()
        packed = jnp.concatenate([v_ref[j], t_ref[j]], axis=1)
        if j < n_peers:
            pk_ref[j] = packed
        else:
            got_ref[d] = packed

    ups = (d + n_row - 1) // n_row
    downs = (2 * n_row - 2 - d) // n_row
    others = (lax.rem(2 * d - z + n_row * n_col, n_col) + n_col - 1) // n_col
    pl.semaphore_wait(barrier, n_peers - 1 + others + n_col - 1 + ups + downs)

    def give(j):
        return pltpu.make_async_remote_copy(
            src_ref=pk_ref.at[j],
            dst_ref=got_ref.at[d],
            send_sem=asend_sem.at[j],
            recv_sem=arecv_sem.at[d],
            device_id={"row": peer(j)},
            device_id_type=MESH,
        )

    def relay(j, o):
        w = peer(j)
        return pltpu.make_async_remote_copy(
            src_ref=got_ref.at[w],
            dst_ref=got_ref.at[w],
            send_sem=rsend_sem.at[o - 1, j],
            recv_sem=arecv_sem.at[w],
            device_id={"col": lax.rem(z + o, n_col)},
            device_id_type=MESH,
        )

    def incoming(w):
        return pltpu.make_async_remote_copy(
            src_ref=got_ref.at[w],
            dst_ref=got_ref.at[w],
            send_sem=rsend_sem.at[0, 0],
            recv_sem=arecv_sem.at[w],
            device_id={"col": lax.rem(z + 1, n_col)},
            device_id_type=MESH,
        )

    def pass_on(j, cond=True):
        @pl.when((peer(j) != d) & cond)
        def _():
            incoming(peer(j)).wait_recv()
            for o in range(1, n_col):
                relay(j, o).start()

    def need(w, cond=True):
        @pl.when((w != d) & (lax.rem(w + d, n_col) != z) & cond)
        def _():
            incoming(w).wait_recv()

    def forward(r):
        return pltpu.make_async_remote_copy(
            src_ref=got_ref.at[2 * r + 1],
            dst_ref=fw_ref.at[r],
            send_sem=fsend_sem.at[r],
            recv_sem=frecv_sem.at[r],
            device_id={"row": d + 1},
            device_id_type=MESH,
        )

    def send_on(r, cond=True):
        need(2 * r + 1, cond)

        @pl.when(has_dn & cond)
        def _():
            forward(r).start()

    def arrive(r, cond=True):
        @pl.when(has_up & cond)
        def _():
            forward(r).wait_recv()

    def link(way, p, c):
        return pltpu.make_async_remote_copy(
            src_ref=cs_ref.at[p, c, pl.ds(way * nb, nb)],
            dst_ref=cr_ref.at[p, c, pl.ds((1 - way) * nb, nb)],
            send_sem=send_sem.at[way, p, c],
            recv_sem=recv_sem.at[way, p, c],
            device_id={"row": d + 2 * way - 1},
            device_id_type=MESH,
        )

    def launch(p, c):
        @pl.when(has_up)
        def _():
            link(0, p, c).start()

        @pl.when(has_dn)
        def _():
            link(1, p, c).start()

    def land(p, c):
        @pl.when(has_up)
        def _():
            link(0, p, c).wait_send()
            link(1, p, c).wait_recv()

        @pl.when(has_dn)
        def _():
            link(1, p, c).wait_send()
            link(0, p, c).wait_recv()

    lane = lax.broadcasted_iota(jnp.int32, (nb, block_rows), 1)
    lane_h = lax.broadcasted_iota(jnp.int32, (nb, half), 1)

    def expanded(block):
        return pltpu.roll(jnp.where(lane < band, block, 0.0), 0, 1, stride=1, stride_axis=0)

    def prepare_even(r):
        block = got_ref[2 * r]
        vh, vl = split(expanded(block))
        on = d >= first_ref[2 * r]
        factor = jnp.where((lane_h >= half - nb) & on, block[:, half:], 0.0)
        th = factor.astype(BF16).astype(F32)
        tl = factor - th
        left = jnp.concatenate([th + pltpu.roll(th, nb, 1), pltpu.roll(tl, nb, 1)], axis=1)
        u = dot(left.astype(BF16), jnp.concatenate([vh, vl, vh, vh], axis=0))
        uh, ul = split(u)
        op = dot_tn(
            jnp.concatenate([vh, vh, vl, jnp.zeros_like(vh)], axis=0),
            jnp.concatenate([uh, ul, uh, uh], axis=0),
        )
        hi, lo = split(op)
        rh_ref[...] = hi
        rl_ref[...] = lo
        return hi, lo

    def prepare_odd(r, oh, ol):
        q = lax.rem(r, 2)
        own = got_ref[2 * r + 1]
        other = fw_ref[r]
        first = first_ref[2 * r + 1]
        none = jnp.zeros((nb, half), F32)
        proj = jnp.concatenate(
            [
                jnp.concatenate([expanded(other)[:, half:], none], axis=1),
                jnp.concatenate([none, expanded(own)[:, :half]], axis=1),
            ],
            axis=0,
        )
        both = jnp.concatenate(
            [
                jnp.where(
                    (lane_h < nb) & (d - 1 >= first), pltpu.roll(other[:, half:], nb, 1), 0.0
                ),
                jnp.where((lane_h >= half - nb) & (d >= first) & has_dn, own[:, half:], 0.0),
            ],
            axis=0,
        )
        ph, pm = split(proj)
        bh, bl = split(both)
        w = dot_tn(
            jnp.concatenate([ph, pm], axis=0), jnp.concatenate([bh, bh], axis=0)
        ) + dot_tn(ph, bl)
        wh, wl = split(w)
        ws_ref[q] = jnp.concatenate([wh, wh], axis=1)
        wl_ref[q] = wl
        s = proj - (dot(ph, oh) + (dot(pm, oh) + dot(ph, ol)))
        sh, sl = split(s)
        sh_ref[...] = sh
        sl_ref[...] = sl
        return sh, sl

    def prepare_link(r, sh, sl):
        q = 1 - lax.rem(r, 2)
        wh = ws_ref[q, :, pl.ds(0, half)]
        h = dot(sh, wh) + (dot(sl, wh) + dot(sh, wl_ref[q]))
        hh, hl = split(h)
        hs_ref[...] = jnp.concatenate([hh, hh], axis=1)
        hl_ref[...] = hl

    def project(y):
        yh, yl = split(y)
        return dot(sh_ref[...], yh) + (dot(sl_ref[...], yh) + dot(sh_ref[...], yl))

    def reflect(x):
        xh, xl = split(x)
        return x - (dot(rh_ref[...], xh) + (dot(rl_ref[...], xh) + dot(rh_ref[...], xl)))

    def corrected(p, c):
        return y_ref[c] - (dot(ws_ref[p], st_ref[c]) + dot(wl_ref[p], st_ref[c, pl.ds(0, half)]))

    def total(p, c):
        th, tl = split(cs_ref[p, c] + cr_ref[p, c])
        st_ref[c] = jnp.concatenate([th, tl], axis=0)

    def columns(c):
        return pl.ds(c * CHUNK, CHUNK)

    turn = d // n_col
    for j in range(n_peers):
        k = lax.rem(j + turn, n_peers)

        @pl.when(peer(k) != d)
        def _():
            give(k).start()

    lead = min(LEAD // n_col, n_peers)
    for j in range(lead):
        pass_on(j)

    send_on(0)
    need(0)
    oh, ol = prepare_even(0)
    for r in range(1, min(AHEAD, rounds)):
        send_on(r)
    arrive(0)
    prepare_odd(0, oh, ol)
    eig_copy.wait()
    for c in range(n_chunks):
        cs_ref[0, c] = project(e_ref[:, columns(c)])
        launch(0, c)

    need(2)
    arrive(1)
    for c in range(n_chunks):
        y_ref[c] = reflect(e_ref[:, columns(c)])
    prepare_link(1, *prepare_odd(1, *prepare_even(1)))
    for c in range(n_chunks):
        g_ref[c] = project(y_ref[c])

    def step(r, carry):
        p = lax.rem(r, 2)
        for c in range(n_chunks):
            land(p, c)
            total(p, c)
            cs_ref[1 - p, c] = g_ref[c] - (
                dot(hs_ref[...], st_ref[c]) + dot(hl_ref[...], st_ref[c, pl.ds(0, half)])
            )
            launch(1 - p, c)

        now = (2 * r + LEAD) // n_col
        pass_on(now, ((2 * r + 2 + LEAD) // n_col > now) & (now < n_peers))
        send_on(r + AHEAD, r + AHEAD < rounds)
        need(2 * r + 4, r + 2 < rounds)
        arrive(r + 2, r + 2 < rounds)

        for c in range(n_chunks):
            y_ref[c] = reflect(corrected(p, c))
        after = jnp.minimum(r + 2, rounds - 1)
        prepare_link(after, *prepare_odd(after, *prepare_even(after)))
        for c in range(n_chunks):
            g_ref[c] = project(y_ref[c])
        return carry

    lax.fori_loop(0, rounds - 1, step, 0)

    p = (rounds - 1) % 2
    for c in range(n_chunks):
        land(p, c)
        total(p, c)
        out_ref[:, columns(c)] = corrected(p, c)

    for j in range(n_peers):

        @pl.when(peer(j) != d)
        def _():
            give(j).wait_send()
            for o in range(1, n_col):
                relay(j, o).wait_send()

    @pl.when(has_dn)
    def _():
        def done(r, carry):
            forward(r).wait_send()
            return carry

        lax.fori_loop(0, rounds, done, 0)


def sweep(eigvecs, reflectors, factors, first_block, n_row, n_col):
    rows = eigvecs.shape[0]
    nb, band = reflectors.shape[2:]
    block_rows = nb + band
    windows = n_row * reflectors.shape[0]
    rounds = windows // 2
    n_chunks = MAX_LIVE // CHUNK
    n_peers = n_row // n_col
    vmem = pltpu.VMEM
    dma = pltpu.SemaphoreType.DMA
    return pl.pallas_call(
        functools.partial(kernel, n_row, n_col),
        out_shape=jax.ShapeDtypeStruct((rows, MAX_LIVE), F32),
        in_specs=[
            pl.BlockSpec(memory_space=pltpu.SMEM),
            pl.BlockSpec(memory_space=pl.ANY),
            pl.BlockSpec(memory_space=pl.ANY),
            pl.BlockSpec(memory_space=pl.ANY),
        ],
        out_specs=pl.BlockSpec(memory_space=pltpu.VMEM),
        scratch_shapes=[
            vmem((rows, MAX_LIVE), F32),
            vmem((n_peers + 1, nb, band), F32),
            vmem((n_peers + 1, nb, nb), F32),
            vmem((n_peers, nb, block_rows), F32),
            vmem((windows, nb, block_rows), F32),
            vmem((rounds, nb, block_rows), F32),
            vmem((n_chunks, rows, CHUNK), F32),
            vmem((n_chunks, 2 * nb, CHUNK), F32),
            vmem((n_chunks, 4 * nb, CHUNK), BF16),
            vmem((2, n_chunks, 2 * nb, CHUNK), F32),
            vmem((2, n_chunks, 2 * nb, CHUNK), F32),
            vmem((rows, rows), BF16),
            vmem((rows, rows), BF16),
            vmem((2 * nb, rows), BF16),
            vmem((2 * nb, rows), BF16),
            vmem((2 * nb, 4 * nb), BF16),
            vmem((2 * nb, 2 * nb), BF16),
            vmem((2, rows, 4 * nb), BF16),
            vmem((2, rows, 2 * nb), BF16),
            dma((2, n_peers + 1)),
            dma,
            dma((n_peers,)),
            dma((max(n_col - 1, 1), n_peers)),
            dma((windows,)),
            dma((2, 2, n_chunks)),
            dma((2, 2, n_chunks)),
            dma((rounds,)),
            dma((rounds,)),
        ],
        compiler_params=pltpu.CompilerParams(
            collective_id=0, has_side_effects=True, vmem_limit_bytes=40 * 2**20
        ),
        name="sweep",
    )(first_block, eigvecs, reflectors, factors)


def body(eigvecs, reflectors, factors, first_block, live_count):
    n_row = lax.axis_size("row")
    n_col = lax.axis_size("col")
    vectors = sweep(eigvecs, reflectors, factors, first_block, n_row, n_col)
    col_count = eigvecs.shape[1]
    vectors = jnp.pad(vectors, ((0, 0), (0, col_count - MAX_LIVE)))
    kept_mask = jnp.arange(col_count, dtype=jnp.int32) < live_count[0]
    return jnp.where(kept_mask[None, :], vectors, 0.0)


def solution(mesh):
    placed = (
        P("row", "col"),
        P("row", None, None, None),
        P("row", None, None, None),
        P(),
        P("col"),
    )
    return jax.shard_map(
        body, mesh=mesh, in_specs=placed, out_specs=P("row", "col"), check_vma=False
    )
```

time: 118 us -> 99.9 us (0.85)
  waiting for transfers between devices: 25.7 us -> 0 us
  Pallas kernels: 77.3 us -> 93.2 us
  starting transfers between devices: 7.74 us -> 0 us
  other arithmetic: 4.82 us -> 1.11 us
  local copies, waits for them, and re-layouts: 1.4 us -> 4.69 us
    all_to_all x1 -> x0, waiting for transfers between devices: 25.7 us -> none  [body(): lax.all_to_all(packed, 'row', split_axis=1, concat_axis=0, tiled=True)]
    pallas_call x1, Pallas kernels: 77.3 us -> 93.2 us  [sweep(): pl.pallas_call(functools.partial(kernel, n_row, n_col), out_shape=jax.Sha...]
    all_to_all x1 -> x0, starting transfers between devices: 7.74 us -> none  [body(): lax.all_to_all(packed, 'row', split_axis=1, concat_axis=0, tiled=True)]
    unnamed x4 -> x8, local copies, waits for them, and re-layouts: 0.01 us -> 4.69 us
    concatenate x1 -> x0, other arithmetic: 1.73 us -> none  [body(): packed = jnp.concatenate([reflectors, factors], axis=3)]
    gather x1 -> x0, local copies, waits for them, and re-layouts: 1.4 us -> none  [body(): applied = block[None, :] >= first_block[window][:, None]]
    select_n x1 -> x0, other arithmetic: 1.36 us -> none  [body(): factors = jnp.where(applied[:, :, None, None], factors, 0.0)]
  transfers between devices with their start and end apart: 1 -> 0, of which waited for: 1 -> 0; matrix products, arithmetic and copies ran while one was open for 0% -> 0% of each run, Pallas kernels for 0% -> 0%
where the time goes in v2:
time: 99.9 us; the launch traced here: 99.6 us
  Pallas kernels  93.2 us (93%)
  local copies, waits for them, and re-layouts  4.69 us (5%)
  other arithmetic  1.11 us (1%)
    pallas_call x1, Pallas kernels, sweep(): pl.pallas_call(functools.partial(kernel, n_row, n_col), out_shape=jax.Sha...  93.2 us
    unnamed x8, local copies, waits for them, and re-layouts  4.69 us

profile of v2, /device:TPU:6, one launch (start us, length us, event | category | flops | bytes accessed | tf_op | source)
XLA Modules:
  0.0 99.6 jit_solution(15055307460679807268)
XLA Ops:
  0.7 0.0 copy-start
  0.7 1.6 %copy-done = f32[1,32,64,192]{3,2,1,0:T(8,128)S(1)} copy-done((f32[1,32,64,192]{3,2,1,0:T(8,128)S(1)}, f32[1,32,64,192]{3,2,1,0:T(8,128)}, u32[]{:S(2)}) %copy-start) | copy-done | bytes 1572888
  2.3 0.0 copy-start.1
  2.3 1.2 %copy-done.1 = f32[256,1024]{1,0:T(8,128)S(1)} copy-done((f32[256,1024]{1,0:T(8,128)S(1)}, f32[256,1024]{1,0:T(8,128)}, u32[]{:S(2)}) %copy-start.1) | copy-done | bytes 1048600
  3.5 0.0 copy-start.2
  3.5 1.2 %copy-done.2 = f32[1,32,64,64]{3,2,1,0:T(8,128)S(1)} copy-done((f32[1,32,64,64]{3,2,1,0:T(8,128)S(1)}, f32[1,32,64,64]{3,2,1,0:T(8,128)}, u32[]{:S(2)}) %copy-start.2) | copy-done | bytes 524312
  4.7 0.0 copy-start.3
  4.7 0.7 copy-done.3
  5.4 93.2 %sweep.1 = f32[256,768]{1,0:T(8,128)S(1)} custom-call(s32[32]{0:T(128)S(1)} %copy-done.3, f32[256,1024]{1,0:T(8,128)S(1)} %copy-done.1, f32[1,32,64,192]{3,2,1,0:T(8,128)S(1)} %copy-done, f32[1,32,64,64]{3,2,1,0:T(8,128)S(1)} %copy-done.2), custom_call_target="tpu_custom_call" | custom-call | tf_op jit(solution)/shard_map/sweep/pallas_call | solution.py:417
  98.5 1.1 %pad_select_fusion = f32[256,1024]{1,0:T(8,128)} fusion(f32[256,768]{1,0:T(8,128)S(1)} %sweep.1, pred[1024]{0:T(1024)(128)(4,1)S(1)} %iota_compare_fusion), kind=kLoop, calls=%fused_computation | loop fusion | flops 262144 | bytes 1836032 | tf_op jit(solution)/shard_map/jit(_where)/select_n | solution.py:471
  (1 shorter events, 0.0 us)
Async XLA Ops:
  0.7 1.6 %copy-start = (f32[1,32,64,192]{3,2,1,0:T(8,128)S(1)}, f32[1,32,64,192]{3,2,1,0:T(8,128)}, u32[]{:S(2)}) copy-start(f32[1,32,64,192]{3,2,1,0:T(8,128)} %refl_hbm.1) | copy-start | bytes 4718596
  2.3 1.2 %copy-start.1 = (f32[256,1024]{1,0:T(8,128)S(1)}, f32[256,1024]{1,0:T(8,128)}, u32[]{:S(2)}) copy-start(f32[256,1024]{1,0:T(8,128)} %eig_hbm.1) | copy-start | bytes 3145732
  3.5 1.2 %copy-start.2 = (f32[1,32,64,64]{3,2,1,0:T(8,128)S(1)}, f32[1,32,64,64]{3,2,1,0:T(8,128)}, u32[]{:S(2)}) copy-start(f32[1,32,64,64]{3,2,1,0:T(8,128)} %fact_hbm.1) | copy-start | bytes 1572868
  4.7 0.7 copy-start.3

commit v3 on v2

--- a/solution.py
+++ b/solution.py
@@ -9,8 +9,10 @@
 
 MAX_LIVE = 768
 CHUNK = 256
-AHEAD = 3
-LEAD = 12
+AHEAD = 4
+LEAD = 16
+FIRST = 8
+SLOTS = 4
 F32 = jnp.float32
 BF16 = jnp.bfloat16
 MESH = pl.DeviceIdType.MESH
@@ -47,15 +49,18 @@
     fw_ref,
     y_ref,
     g_ref,
+    d_ref,
     st_ref,
     cs_ref,
     cr_ref,
+    hsend_ref,
+    hrecv_ref,
     rh_ref,
     rl_ref,
     sh_ref,
     sl_ref,
-    hs_ref,
-    hl_ref,
+    ho_ref,
+    hd_ref,
     ws_ref,
     wl_ref,
     local_sem,
@@ -67,11 +72,11 @@
     recv_sem,
     fsend_sem,
     frecv_sem,
+    hsend_sem,
+    hrecv_sem,
 ):
     d = lax.axis_index("row")
     z = lax.axis_index("col")
-    has_up = d > 0
-    has_dn = d < n_row - 1
     windows, nb, block_rows = got_ref.shape
     band = block_rows - nb
     rounds = windows // 2
@@ -80,6 +85,19 @@
     n_peers = n_row // n_col
     kin = lax.rem(z - d + n_row * n_col, n_col)
 
+    odd = lax.rem(d, 2)
+    is_odd = odd == 1
+    has_up = d > 0
+    has_dn = d < n_row - 1
+    has_edge = (has_up & has_dn, None)
+    across = (d - 1 + 2 * odd, d + 1 - 2 * odd)
+
+    def only(cond, todo):
+        if cond is None:
+            todo()
+        else:
+            pl.when(cond)(todo)
+
     def peer(j):
         return kin + n_col * j
 
@@ -117,15 +135,14 @@
     @pl.when(jnp.logical_not(has_up))
     def _():
         fw_ref[...] = jnp.zeros_like(fw_ref)
-        for p in range(2):
+
+    @pl.when(jnp.logical_not(has_edge[0]))
+    def _():
+        for r in range(rounds):
+            hrecv_ref[r, 0] = jnp.zeros((nb // 2, half), F32)
+        for p in range(SLOTS):
             for c in range(n_chunks):
-                cr_ref[p, c, pl.ds(0, nb)] = jnp.zeros((nb, CHUNK), F32)
-
-    @pl.when(jnp.logical_not(has_dn))
-    def _():
-        for p in range(2):
-            for c in range(n_chunks):
-                cr_ref[p, c, pl.ds(nb, nb)] = jnp.zeros((nb, CHUNK), F32)
+                cr_ref[p, c, 0] = jnp.zeros((nb, CHUNK), F32)
 
     for j in range(n_peers + 1):
         for copy in fetch(j):
@@ -206,50 +223,51 @@
         def _():
             forward(r).wait_recv()
 
-    def link(way, p, c):
+    def link(k, p, c):
         return pltpu.make_async_remote_copy(
-            src_ref=cs_ref.at[p, c, pl.ds(way * nb, nb)],
-            dst_ref=cr_ref.at[p, c, pl.ds((1 - way) * nb, nb)],
-            send_sem=send_sem.at[way, p, c],
-            recv_sem=recv_sem.at[way, p, c],
-            device_id={"row": d + 2 * way - 1},
+            src_ref=cs_ref.at[p, c, k],
+            dst_ref=cr_ref.at[p, c, k],
+            send_sem=send_sem.at[k, p, c],
+            recv_sem=recv_sem.at[k, p, c],
+            device_id={"row": across[k]},
             device_id_type=MESH,
         )
 
-    def launch(p, c):
-        @pl.when(has_up)
-        def _():
-            link(0, p, c).start()
-
-        @pl.when(has_dn)
-        def _():
-            link(1, p, c).start()
-
-    def land(p, c):
-        @pl.when(has_up)
-        def _():
-            link(0, p, c).wait_send()
-            link(1, p, c).wait_recv()
-
-        @pl.when(has_dn)
-        def _():
-            link(1, p, c).wait_send()
-            link(0, p, c).wait_recv()
+    def launch(k, p, c):
+        only(has_edge[k], lambda: link(k, p, c).start())
+
+    def land(k, p, c):
+        only(has_edge[k], lambda: link(k, p, c).wait())
+
+    def swap(k, r):
+        return pltpu.make_async_remote_copy(
+            src_ref=hsend_ref.at[r, k],
+            dst_ref=hrecv_ref.at[r, k],
+            send_sem=hsend_sem.at[k, r],
+            recv_sem=hrecv_sem.at[k, r],
+            device_id={"row": across[k]},
+            device_id_type=MESH,
+        )
 
     lane = lax.broadcasted_iota(jnp.int32, (nb, block_rows), 1)
     lane_h = lax.broadcasted_iota(jnp.int32, (nb, half), 1)
+    lane_q = lax.broadcasted_iota(jnp.int32, (nb // 2, half), 1)
+    low, high = lane_h < nb, lane_h >= nb
+
+    def turned(x):
+        return pltpu.roll(x, nb, 1)
 
     def expanded(block):
         return pltpu.roll(jnp.where(lane < band, block, 0.0), 0, 1, stride=1, stride_axis=0)
 
-    def prepare_even(r):
+    def prepare_even(r, q):
         block = got_ref[2 * r]
         vh, vl = split(expanded(block))
         on = d >= first_ref[2 * r]
-        factor = jnp.where((lane_h >= half - nb) & on, block[:, half:], 0.0)
+        factor = jnp.where(high & on, block[:, half:], 0.0)
         th = factor.astype(BF16).astype(F32)
         tl = factor - th
-        left = jnp.concatenate([th + pltpu.roll(th, nb, 1), pltpu.roll(tl, nb, 1)], axis=1)
+        left = jnp.concatenate([th + turned(th), turned(tl)], axis=1)
         u = dot(left.astype(BF16), jnp.concatenate([vh, vl, vh, vh], axis=0))
         uh, ul = split(u)
         op = dot_tn(
@@ -257,29 +275,26 @@
             jnp.concatenate([uh, ul, uh, uh], axis=0),
         )
         hi, lo = split(op)
-        rh_ref[...] = hi
-        rl_ref[...] = lo
+        rh_ref[q] = hi
+        rl_ref[q] = lo
         return hi, lo
 
-    def prepare_odd(r, oh, ol):
-        q = lax.rem(r, 2)
+    def prepare_odd(r, q, oh, ol):
         own = got_ref[2 * r + 1]
         other = fw_ref[r]
         first = first_ref[2 * r + 1]
         none = jnp.zeros((nb, half), F32)
+        upper = jnp.concatenate([expanded(other)[:, half:], none], axis=1)
+        lower = jnp.concatenate([none, expanded(own)[:, :half]], axis=1)
         proj = jnp.concatenate(
-            [
-                jnp.concatenate([expanded(other)[:, half:], none], axis=1),
-                jnp.concatenate([none, expanded(own)[:, :half]], axis=1),
-            ],
-            axis=0,
-        )
+            [jnp.where(is_odd, lower, upper), jnp.where(is_odd, upper, lower)], axis=0
+        )
+        t_up = jnp.where(d - 1 >= first, other[:, half:], 0.0)
+        t_dn = jnp.where((d >= first) & has_dn, own[:, half:], 0.0)
         both = jnp.concatenate(
             [
-                jnp.where(
-                    (lane_h < nb) & (d - 1 >= first), pltpu.roll(other[:, half:], nb, 1), 0.0
-                ),
-                jnp.where((lane_h >= half - nb) & (d >= first) & has_dn, own[:, half:], 0.0),
+                jnp.where(low, turned(jnp.where(is_odd, t_dn, t_up)), 0.0),
+                jnp.where(high, jnp.where(is_odd, t_up, t_dn), 0.0),
             ],
             axis=0,
         )
@@ -293,98 +308,172 @@
         wl_ref[q] = wl
         s = proj - (dot(ph, oh) + (dot(pm, oh) + dot(ph, ol)))
         sh, sl = split(s)
-        sh_ref[...] = sh
-        sl_ref[...] = sl
+        sh_ref[q] = sh
+        sl_ref[q] = sl
         return sh, sl
 
-    def prepare_link(r, sh, sl):
-        q = 1 - lax.rem(r, 2)
-        wh = ws_ref[q, :, pl.ds(0, half)]
-        h = dot(sh, wh) + (dot(sl, wh) + dot(sh, wl_ref[q]))
-        hh, hl = split(h)
-        hs_ref[...] = jnp.concatenate([hh, hh], axis=1)
-        hl_ref[...] = hl
-
-    def project(y):
+    def prepare_link(q, at, sh, sl):
+        b = lax.rem(q + SLOTS - 1, SLOTS)
+        wh = ws_ref[b, :, pl.ds(0, half)]
+        h = dot(sh, wh) + (dot(sl, wh) + dot(sh, wl_ref[b]))
+        top, bottom = h[:nb], h[nb:]
+        th = top.astype(BF16).astype(F32)
+        hi, lo = jnp.where(high, th, 0.0), jnp.where(high, top - th, 0.0)
+        ho_ref[q, 0] = jnp.concatenate([hi + turned(hi), turned(lo)], axis=1).astype(BF16)
+        bh = bottom.astype(BF16).astype(F32)
+        hi, lo = jnp.where(low, bh, 0.0), jnp.where(low, bottom - bh, 0.0)
+        ho_ref[q, 1] = jnp.concatenate([hi + turned(hi), lo], axis=1).astype(BF16)
+        hd_ref[q, pl.ds(0, nb)] = jnp.where(low, top, 0.0)
+        hd_ref[q, pl.ds(nb, nb)] = jnp.where(high, bottom, 0.0)
+        quarter = nb // 2
+        hsend_ref[at, 0] = jnp.where(lane_q < nb, top[:quarter], turned(top[quarter:]))
+        hsend_ref[at, 1] = jnp.where(lane_q < nb, turned(bottom[:quarter]), bottom[quarter:])
+
+    def swap_start(r, cond=True):
+        for k in range(2):
+            have = cond if has_edge[k] is None else has_edge[k] & cond
+            only(None if have is True else have, lambda k=k: swap(k, r).start())
+
+    def diagonal(r, q):
+        x, s = hrecv_ref[r, 0], hrecv_ref[r, 1]
+        left, right = lane_q < nb, lane_q >= nb
+        total = hd_ref[q] + jnp.concatenate(
+            [
+                jnp.where(left, x, 0.0),
+                jnp.where(left, turned(x), 0.0),
+                jnp.where(right, turned(s), 0.0),
+                jnp.where(right, s, 0.0),
+            ],
+            axis=0,
+        )
+        hi, lo = split(total)
+        return jnp.concatenate([hi, hi], axis=1), lo
+
+    def prepare(r, q, at):
+        sh, sl = prepare_odd(r, q, *prepare_even(r, q))
+        prepare_link(q, at, sh, sl)
+
+    def project(y, q):
         yh, yl = split(y)
-        return dot(sh_ref[...], yh) + (dot(sl_ref[...], yh) + dot(sh_ref[...], yl))
-
-    def reflect(x):
+        return dot(sh_ref[q], yh) + (dot(sl_ref[q], yh) + dot(sh_ref[q], yl))
+
+    def reflect(x, q):
         xh, xl = split(x)
-        return x - (dot(rh_ref[...], xh) + (dot(rl_ref[...], xh) + dot(rh_ref[...], xl)))
-
-    def corrected(p, c):
-        return y_ref[c] - (dot(ws_ref[p], st_ref[c]) + dot(wl_ref[p], st_ref[c, pl.ds(0, half)]))
-
-    def total(p, c):
-        th, tl = split(cs_ref[p, c] + cr_ref[p, c])
-        st_ref[c] = jnp.concatenate([th, tl], axis=0)
+        return x - (dot(rh_ref[q], xh) + (dot(rl_ref[q], xh) + dot(rh_ref[q], xl)))
+
+    def corrected(q, c):
+        return y_ref[c] - (dot(ws_ref[q], st_ref[c]) + dot(wl_ref[q], st_ref[c, pl.ds(0, half)]))
+
+    def total(k, p, c):
+        at = k * nb
+        th, tl = split(d_ref[c, pl.ds(at, nb)] + cr_ref[p, c, k])
+        st_ref[c, pl.ds(at, nb)] = th
+        st_ref[c, pl.ds(half + at, nb)] = tl
+        return th, tl
+
+    def answer(k, p, n, c):
+        land(k, p, c)
+        th, tl = total(k, p, c)
+        cs_ref[n, c, 1 - k] = g_ref[c, pl.ds((1 - k) * nb, nb)] - dot(
+            ho_ref[n, 1 - k], jnp.concatenate([th, tl, th, th], axis=0)
+        )
+        launch(1 - k, n, c)
 
     def columns(c):
         return pl.ds(c * CHUNK, CHUNK)
 
-    turn = d // n_col
-    for j in range(n_peers):
-        k = lax.rem(j + turn, n_peers)
-
-        @pl.when(peer(k) != d)
-        def _():
-            give(k).start()
+    def give_all():
+        turn = d // n_col
+        for j in range(n_peers):
+            i = lax.rem(j + turn, n_peers)
+
+            @pl.when(peer(i) != d)
+            def _():
+                give(i).start()
+
+    early = d < FIRST
+
+    @pl.when(early)
+    def _():
+        give_all()
 
     lead = min(LEAD // n_col, n_peers)
-    for j in range(lead):
+    soon = min(FIRST // n_col, lead)
+    for j in range(soon):
         pass_on(j)
+
+    @pl.when(jnp.logical_not(early))
+    def _():
+        give_all()
 
     send_on(0)
     need(0)
-    oh, ol = prepare_even(0)
-    for r in range(1, min(AHEAD, rounds)):
-        send_on(r)
+    ops = prepare_even(0, 0)
     arrive(0)
-    prepare_odd(0, oh, ol)
+    prepare_odd(0, 0, *ops)
     eig_copy.wait()
     for c in range(n_chunks):
-        cs_ref[0, c] = project(e_ref[:, columns(c)])
-        launch(0, c)
-
-    need(2)
-    arrive(1)
+        x = project(e_ref[:, columns(c)], 0)
+        d_ref[c] = x
+        for k in range(2):
+            cs_ref[0, c, k] = x[k * nb : (k + 1) * nb]
+            launch(k, 0, c)
+
+    for r in range(1, min(3, rounds)):
+        send_on(r)
+        need(2 * r)
     for c in range(n_chunks):
-        y_ref[c] = reflect(e_ref[:, columns(c)])
-    prepare_link(1, *prepare_odd(1, *prepare_even(1)))
+        y_ref[c] = reflect(e_ref[:, columns(c)], 0)
+    for r in range(1, min(3, rounds)):
+        arrive(r)
+        prepare(r, r, r)
+        swap_start(r)
     for c in range(n_chunks):
-        g_ref[c] = project(y_ref[c])
+        g_ref[c] = project(y_ref[c], 1)
+    for j in range(soon, lead):
+        pass_on(j)
+    for r in range(3, min(AHEAD, rounds)):
+        send_on(r)
 
     def step(r, carry):
-        p = lax.rem(r, 2)
+        p = lax.rem(r, SLOTS)
+        n = lax.rem(r + 1, SLOTS)
         for c in range(n_chunks):
-            land(p, c)
-            total(p, c)
-            cs_ref[1 - p, c] = g_ref[c] - (
-                dot(hs_ref[...], st_ref[c]) + dot(hl_ref[...], st_ref[c, pl.ds(0, half)])
-            )
-            launch(1 - p, c)
+            answer(1, p, n, c)
 
         now = (2 * r + LEAD) // n_col
         pass_on(now, ((2 * r + 2 + LEAD) // n_col > now) & (now < n_peers))
         send_on(r + AHEAD, r + AHEAD < rounds)
-        need(2 * r + 4, r + 2 < rounds)
-        arrive(r + 2, r + 2 < rounds)
+        later = r + 3 < rounds
+        need(2 * r + 6, later)
+        arrive(r + 3, later)
+        after = jnp.minimum(r + 3, rounds - 1)
+        prepare(after, lax.rem(r + 3, SLOTS), r + 3)
+        swap_start(r + 3, later)
 
         for c in range(n_chunks):
-            y_ref[c] = reflect(corrected(p, c))
-        after = jnp.minimum(r + 2, rounds - 1)
-        prepare_link(after, *prepare_odd(after, *prepare_even(after)))
+            answer(0, p, n, c)
+
+        for k in range(2):
+            only(has_edge[k], lambda k=k: swap(k, r + 1).wait())
+        both, low_part = diagonal(r + 1, n)
         for c in range(n_chunks):
-            g_ref[c] = project(y_ref[c])
+            y_ref[c] = reflect(corrected(p, c), n)
+        for c in range(n_chunks):
+            g_ref[c] = project(y_ref[c], lax.rem(r + 2, SLOTS))
+        for c in range(n_chunks):
+            less = dot(both, st_ref[c]) + dot(low_part, st_ref[c, pl.ds(0, half)])
+            for k in range(2):
+                d_ref[c, pl.ds(k * nb, nb)] = cs_ref[n, c, k] - less[k * nb : (k + 1) * nb]
         return carry
 
     lax.fori_loop(0, rounds - 1, step, 0)
 
-    p = (rounds - 1) % 2
+    p = (rounds - 1) % SLOTS
     for c in range(n_chunks):
-        land(p, c)
-        total(p, c)
+        for k in (1, 0):
+            land(k, p, c)
+            total(k, p, c)
         out_ref[:, columns(c)] = corrected(p, c)
 
     for j in range(n_peers):
@@ -414,15 +503,11 @@
     n_peers = n_row // n_col
     vmem = pltpu.VMEM
     dma = pltpu.SemaphoreType.DMA
+    hbm = pl.BlockSpec(memory_space=pltpu.HBM)
     return pl.pallas_call(
         functools.partial(kernel, n_row, n_col),
         out_shape=jax.ShapeDtypeStruct((rows, MAX_LIVE), F32),
-        in_specs=[
-            pl.BlockSpec(memory_space=pltpu.SMEM),
-            pl.BlockSpec(memory_space=pl.ANY),
-            pl.BlockSpec(memory_space=pl.ANY),
-            pl.BlockSpec(memory_space=pl.ANY),
-        ],
+        in_specs=[pl.BlockSpec(memory_space=pltpu.SMEM), hbm, hbm, hbm],
         out_specs=pl.BlockSpec(memory_space=pltpu.VMEM),
         scratch_shapes=[
             vmem((rows, MAX_LIVE), F32),
@@ -433,30 +518,33 @@
             vmem((rounds, nb, block_rows), F32),
             vmem((n_chunks, rows, CHUNK), F32),
             vmem((n_chunks, 2 * nb, CHUNK), F32),
+            vmem((n_chunks, 2 * nb, CHUNK), F32),
             vmem((n_chunks, 4 * nb, CHUNK), BF16),
-            vmem((2, n_chunks, 2 * nb, CHUNK), F32),
-            vmem((2, n_chunks, 2 * nb, CHUNK), F32),
-            vmem((rows, rows), BF16),
-            vmem((rows, rows), BF16),
-            vmem((2 * nb, rows), BF16),
-            vmem((2 * nb, rows), BF16),
-            vmem((2 * nb, 4 * nb), BF16),
-            vmem((2 * nb, 2 * nb), BF16),
-            vmem((2, rows, 4 * nb), BF16),
-            vmem((2, rows, 2 * nb), BF16),
+            vmem((SLOTS, n_chunks, 2, nb, CHUNK), F32),
+            vmem((SLOTS, n_chunks, 2, nb, CHUNK), F32),
+            vmem((rounds + 3, 2, nb // 2, 2 * nb), F32),
+            vmem((rounds, 2, nb // 2, 2 * nb), F32),
+            vmem((SLOTS, rows, rows), BF16),
+            vmem((SLOTS, rows, rows), BF16),
+            vmem((SLOTS, 2 * nb, rows), BF16),
+            vmem((SLOTS, 2 * nb, rows), BF16),
+            vmem((SLOTS, 2, nb, 4 * nb), BF16),
+            vmem((SLOTS, 2 * nb, 2 * nb), F32),
+            vmem((SLOTS, rows, 4 * nb), BF16),
+            vmem((SLOTS, rows, 2 * nb), BF16),
             dma((2, n_peers + 1)),
             dma,
             dma((n_peers,)),
             dma((max(n_col - 1, 1), n_peers)),
             dma((windows,)),
-            dma((2, 2, n_chunks)),
-            dma((2, 2, n_chunks)),
+            dma((2, SLOTS, n_chunks)),
+            dma((2, SLOTS, n_chunks)),
             dma((rounds,)),
             dma((rounds,)),
+            dma((2, rounds)),
+            dma((2, rounds)),
         ],
-        compiler_params=pltpu.CompilerParams(
-            collective_id=0, has_side_effects=True, vmem_limit_bytes=40 * 2**20
-        ),
+        compiler_params=pltpu.CompilerParams(collective_id=0, has_side_effects=True),
         name="sweep",
     )(first_block, eigvecs, reflectors, factors)
 

time: 99.9 us -> 99.1 us (level)
  local copies, waits for them, and re-layouts: 4.69 us -> 0 us
  Pallas kernels: 93.2 us -> 95.1 us
  other arithmetic: 1.11 us -> 2.23 us
    unnamed x8 -> x0, local copies, waits for them, and re-layouts: 4.69 us -> none
    pallas_call x1, Pallas kernels: 93.2 us -> 95.1 us  [sweep(): pl.pallas_call(functools.partial(kernel, n_row, n_col), out_shape=jax.Sha...]
    select_n x1, other arithmetic: 1.1 us -> 2.23 us  [body(): return jnp.where(kept_mask[None, :], vectors, 0.0)]
where the time goes in v3:
time: 99.1 us; the launch traced here: 98 us
  Pallas kernels  95.1 us (96%)
  other arithmetic  2.23 us (2%)
    pallas_call x1, Pallas kernels, sweep(): pl.pallas_call(functools.partial(kernel, n_row, n_col), out_shape=jax.Sha...  95.1 us
    select_n x1, other arithmetic, body(): return jnp.where(kept_mask[None, :], vectors, 0.0)  2.23 us

profile of v3, /device:TPU:6, one launch (start us, length us, event | category | flops | bytes accessed | tf_op | source)
XLA Modules:
  0.0 98.0 jit_solution(12779384222641123490)
XLA Ops:
  0.7 95.1 %sweep.1 = f32[256,768]{1,0:T(8,128)} custom-call(s32[32]{0:T(128)} %first_ref.1, f32[256,1024]{1,0:T(8,128)} %eig_hbm.1, f32[1,32,64,192]{3,2,1,0:T(8,128)} %refl_hbm.1, f32[1,32,64,64]{3,2,1,0:T(8,128)} %fact_hbm.1), custom_call_target="tpu_custom_call" | custom-call | tf_op jit(solution)/shard_map/sweep/pallas_call | solution.py:507
  95.8 2.2 %pad_select_fusion = f32[256,1024]{1,0:T(8,128)} fusion(f32[256,768]{1,0:T(8,128)} %sweep.1, pred[1024]{0:T(1024)(128)(4,1)S(1)} %iota_compare_fusion), kind=kLoop, calls=%fused_computation | loop fusion | flops 262144 | bytes 1836032 | tf_op jit(solution)/shard_map/jit(_where)/select_n | solution.py:559
  (1 shorter events, 0.0 us)

commit v4 on v3

--- a/solution.py
+++ b/solution.py
@@ -13,6 +13,7 @@
 LEAD = 16
 FIRST = 8
 SLOTS = 4
+RING = 8
 F32 = jnp.float32
 BF16 = jnp.bfloat16
 MESH = pl.DeviceIdType.MESH
@@ -50,7 +51,6 @@
     y_ref,
     g_ref,
     d_ref,
-    st_ref,
     cs_ref,
     cr_ref,
     hsend_ref,
@@ -59,10 +59,10 @@
     rl_ref,
     sh_ref,
     sl_ref,
-    ho_ref,
     hd_ref,
-    ws_ref,
+    wh_ref,
     wl_ref,
+    op_ref,
     local_sem,
     eig_sem,
     asend_sem,
@@ -117,16 +117,15 @@
     greet(has_up, {"row": d - 1})
     greet(has_dn, {"row": d + 1})
 
-    def fetch(j):
-        t = peer(j) if j < n_peers else d
-        return (
-            pltpu.make_async_copy(refl_hbm.at[0, t], v_ref.at[j], local_sem.at[0, j]),
-            pltpu.make_async_copy(fact_hbm.at[0, t], t_ref.at[j], local_sem.at[1, j]),
-        )
-
-    for j in range(n_peers + 1):
-        for copy in fetch(j):
-            copy.start()
+    at, within = d // n_col, lax.rem(d, n_col)
+    fetches = [
+        pltpu.make_async_copy(refl_hbm.at[:, kin], v_ref.at[pl.ds(0, n_peers)], local_sem.at[0]),
+        pltpu.make_async_copy(fact_hbm.at[:, kin], t_ref.at[pl.ds(0, n_peers)], local_sem.at[1]),
+        pltpu.make_async_copy(refl_hbm.at[at, within], v_ref.at[n_peers], local_sem.at[2]),
+        pltpu.make_async_copy(fact_hbm.at[at, within], t_ref.at[n_peers], local_sem.at[3]),
+    ]
+    for copy in fetches:
+        copy.start()
     eig_copy = pltpu.make_async_copy(
         eig_hbm.at[:, pl.ds(0, n_chunks * CHUNK)], e_ref, eig_sem
     )
@@ -144,9 +143,9 @@
             for c in range(n_chunks):
                 cr_ref[p, c, 0] = jnp.zeros((nb, CHUNK), F32)
 
+    for copy in fetches:
+        copy.wait()
     for j in range(n_peers + 1):
-        for copy in fetch(j):
-            copy.wait()
         packed = jnp.concatenate([v_ref[j], t_ref[j]], axis=1)
         if j < n_peers:
             pk_ref[j] = packed
@@ -162,7 +161,7 @@
         return pltpu.make_async_remote_copy(
             src_ref=pk_ref.at[j],
             dst_ref=got_ref.at[d],
-            send_sem=asend_sem.at[j],
+            send_sem=asend_sem,
             recv_sem=arecv_sem.at[d],
             device_id={"row": peer(j)},
             device_id_type=MESH,
@@ -173,7 +172,7 @@
         return pltpu.make_async_remote_copy(
             src_ref=got_ref.at[w],
             dst_ref=got_ref.at[w],
-            send_sem=rsend_sem.at[o - 1, j],
+            send_sem=rsend_sem,
             recv_sem=arecv_sem.at[w],
             device_id={"col": lax.rem(z + o, n_col)},
             device_id_type=MESH,
@@ -183,7 +182,7 @@
         return pltpu.make_async_remote_copy(
             src_ref=got_ref.at[w],
             dst_ref=got_ref.at[w],
-            send_sem=rsend_sem.at[0, 0],
+            send_sem=rsend_sem,
             recv_sem=arecv_sem.at[w],
             device_id={"col": lax.rem(z + 1, n_col)},
             device_id_type=MESH,
@@ -205,8 +204,8 @@
         return pltpu.make_async_remote_copy(
             src_ref=got_ref.at[2 * r + 1],
             dst_ref=fw_ref.at[r],
-            send_sem=fsend_sem.at[r],
-            recv_sem=frecv_sem.at[r],
+            send_sem=fsend_sem,
+            recv_sem=frecv_sem.at[lax.rem(r, RING)],
             device_id={"row": d + 1},
             device_id_type=MESH,
         )
@@ -243,8 +242,8 @@
         return pltpu.make_async_remote_copy(
             src_ref=hsend_ref.at[r, k],
             dst_ref=hrecv_ref.at[r, k],
-            send_sem=hsend_sem.at[k, r],
-            recv_sem=hrecv_sem.at[k, r],
+            send_sem=hsend_sem.at[k],
+            recv_sem=hrecv_sem.at[k, lax.rem(r, RING)],
             device_id={"row": across[k]},
             device_id_type=MESH,
         )
@@ -253,6 +252,7 @@
     lane_h = lax.broadcasted_iota(jnp.int32, (nb, half), 1)
     lane_q = lax.broadcasted_iota(jnp.int32, (nb // 2, half), 1)
     low, high = lane_h < nb, lane_h >= nb
+    wide = lax.broadcasted_iota(jnp.int32, (half, half), 1) < nb
 
     def turned(x):
         return pltpu.roll(x, nb, 1)
@@ -279,33 +279,43 @@
         rl_ref[q] = lo
         return hi, lo
 
+    def stacked(x):
+        hi = x.astype(BF16)
+        lo = jnp.where(low, x - hi.astype(F32), 0.0).astype(BF16)
+        return jnp.concatenate([hi, lo], axis=1)
+
     def prepare_odd(r, q, oh, ol):
         own = got_ref[2 * r + 1]
         other = fw_ref[r]
         first = first_ref[2 * r + 1]
         none = jnp.zeros((nb, half), F32)
-        upper = jnp.concatenate([expanded(other)[:, half:], none], axis=1)
-        lower = jnp.concatenate([none, expanded(own)[:, :half]], axis=1)
-        proj = jnp.concatenate(
-            [jnp.where(is_odd, lower, upper), jnp.where(is_odd, upper, lower)], axis=0
-        )
-        t_up = jnp.where(d - 1 >= first, other[:, half:], 0.0)
-        t_dn = jnp.where((d >= first) & has_dn, own[:, half:], 0.0)
-        both = jnp.concatenate(
-            [
-                jnp.where(low, turned(jnp.where(is_odd, t_dn, t_up)), 0.0),
-                jnp.where(high, jnp.where(is_odd, t_up, t_dn), 0.0),
-            ],
-            axis=0,
-        )
+        up, dn = expanded(other)[:, half:], expanded(own)[:, :half]
+        t_up = jnp.where(high & (d - 1 >= first), other[:, half:], 0.0)
+        t_dn = jnp.where(high & (d >= first) & has_dn, own[:, half:], 0.0)
+        rows = []
+        for k in range(2):
+            flip = is_odd if k == 0 else jnp.logical_not(is_odd)
+            part = jnp.where(flip, dn, up)
+            rows.append(
+                jnp.concatenate(
+                    [jnp.where(flip, none, part), jnp.where(flip, part, none)], axis=1
+                )
+            )
+            factor = jnp.where(flip, t_dn, t_up)
+            ph, pm = split(part)
+            fh, fm = split(factor + turned(factor))
+            w = dot_tn(
+                jnp.concatenate([ph, ph, pm, jnp.zeros_like(ph)], axis=0),
+                jnp.concatenate([fh, fm, fh, fh], axis=0),
+            )
+            wh, wl = split(w)
+            wh_ref[q, k] = wh
+            wl_ref[q, k] = wl
+            op_ref[q, k, pl.ds(half, half)] = jnp.concatenate(
+                [wh, jnp.where(wide, wl.astype(F32), 0.0).astype(BF16)], axis=1
+            )
+        proj = jnp.concatenate(rows, axis=0)
         ph, pm = split(proj)
-        bh, bl = split(both)
-        w = dot_tn(
-            jnp.concatenate([ph, pm], axis=0), jnp.concatenate([bh, bh], axis=0)
-        ) + dot_tn(ph, bl)
-        wh, wl = split(w)
-        ws_ref[q] = jnp.concatenate([wh, wh], axis=1)
-        wl_ref[q] = wl
         s = proj - (dot(ph, oh) + (dot(pm, oh) + dot(ph, ol)))
         sh, sl = split(s)
         sh_ref[q] = sh
@@ -314,40 +324,37 @@
 
     def prepare_link(q, at, sh, sl):
         b = lax.rem(q + SLOTS - 1, SLOTS)
-        wh = ws_ref[b, :, pl.ds(0, half)]
-        h = dot(sh, wh) + (dot(sl, wh) + dot(sh, wl_ref[b]))
-        top, bottom = h[:nb], h[nb:]
-        th = top.astype(BF16).astype(F32)
-        hi, lo = jnp.where(high, th, 0.0), jnp.where(high, top - th, 0.0)
-        ho_ref[q, 0] = jnp.concatenate([hi + turned(hi), turned(lo)], axis=1).astype(BF16)
-        bh = bottom.astype(BF16).astype(F32)
-        hi, lo = jnp.where(low, bh, 0.0), jnp.where(low, bottom - bh, 0.0)
-        ho_ref[q, 1] = jnp.concatenate([hi + turned(hi), lo], axis=1).astype(BF16)
-        hd_ref[q, pl.ds(0, nb)] = jnp.where(low, top, 0.0)
-        hd_ref[q, pl.ds(nb, nb)] = jnp.where(high, bottom, 0.0)
         quarter = nb // 2
-        hsend_ref[at, 0] = jnp.where(lane_q < nb, top[:quarter], turned(top[quarter:]))
-        hsend_ref[at, 1] = jnp.where(lane_q < nb, turned(bottom[:quarter]), bottom[quarter:])
+        for k in range(2):
+            flip = is_odd if k == 0 else jnp.logical_not(is_odd)
+            ah = jnp.where(flip, sh[:, half:].astype(F32), sh[:, :half].astype(F32)).astype(BF16)
+            al = jnp.where(flip, sl[:, half:].astype(F32), sl[:, :half].astype(F32)).astype(BF16)
+            wh = wh_ref[b, k]
+            h = dot(
+                jnp.concatenate([ah, al], axis=1), jnp.concatenate([wh, wh], axis=0)
+            ) + dot(ah, wl_ref[b, k])
+            here, there = h[k * nb : (k + 1) * nb], h[(1 - k) * nb : (2 - k) * nb]
+            op_ref[b, k, pl.ds(0, nb)] = stacked(there)
+            hd_ref[q, k] = here
+            hsend_ref[at, k] = jnp.where(lane_q < nb, here[:quarter], here[quarter:])
 
     def swap_start(r, cond=True):
         for k in range(2):
             have = cond if has_edge[k] is None else has_edge[k] & cond
             only(None if have is True else have, lambda k=k: swap(k, r).start())
 
-    def diagonal(r, q):
-        x, s = hrecv_ref[r, 0], hrecv_ref[r, 1]
-        left, right = lane_q < nb, lane_q >= nb
-        total = hd_ref[q] + jnp.concatenate(
-            [
-                jnp.where(left, x, 0.0),
-                jnp.where(left, turned(x), 0.0),
-                jnp.where(right, turned(s), 0.0),
-                jnp.where(right, s, 0.0),
-            ],
-            axis=0,
-        )
-        hi, lo = split(total)
-        return jnp.concatenate([hi, hi], axis=1), lo
+    def combine(r, q, cond=True):
+        b = lax.rem(q + SLOTS - 1, SLOTS)
+        for k in range(2):
+            have = cond if has_edge[k] is None else has_edge[k] & cond
+            only(None if have is True else have, lambda k=k: swap(k, r).wait_recv())
+        for k in range(2):
+            x = hrecv_ref[r, k]
+            left = lane_q < nb
+            theirs = jnp.concatenate(
+                [jnp.where(left, x, turned(x)), jnp.where(left, turned(x), x)], axis=0
+            )
+            op_ref[b, k, pl.ds(nb, nb)] = stacked(hd_ref[q, k] + theirs)
 
     def prepare(r, q, at):
         sh, sl = prepare_odd(r, q, *prepare_even(r, q))
@@ -361,23 +368,25 @@
         xh, xl = split(x)
         return x - (dot(rh_ref[q], xh) + (dot(rl_ref[q], xh) + dot(rh_ref[q], xl)))
 
-    def corrected(q, c):
-        return y_ref[c] - (dot(ws_ref[q], st_ref[c]) + dot(wl_ref[q], st_ref[c, pl.ds(0, half)]))
-
     def total(k, p, c):
-        at = k * nb
-        th, tl = split(d_ref[c, pl.ds(at, nb)] + cr_ref[p, c, k])
-        st_ref[c, pl.ds(at, nb)] = th
-        st_ref[c, pl.ds(half + at, nb)] = tl
-        return th, tl
+        th, tl = split(d_ref[c, k] + cr_ref[p, c, k])
+        return jnp.concatenate([th, tl, th, th], axis=0)
+
+    def side(k):
+        h = odd if k == 0 else 1 - odd
+        return pl.ds(pl.multiple_of(h * half, half), half)
 
     def answer(k, p, n, c):
-        land(k, p, c)
-        th, tl = total(k, p, c)
-        cs_ref[n, c, 1 - k] = g_ref[c, pl.ds((1 - k) * nb, nb)] - dot(
-            ho_ref[n, 1 - k], jnp.concatenate([th, tl, th, th], axis=0)
-        )
+        res = dot(op_ref[p, k], total(k, p, c))
+        x = g_ref[c, 1 - k] - res[:nb]
+        cs_ref[n, c, 1 - k] = x
         launch(1 - k, n, c)
+        y_ref[c, side(k)] = y_ref[c, side(k)] - res[half:]
+        if k == 1:
+            d_ref[c, 1] = res[nb:half]
+        else:
+            d_ref[c, 1] = x - d_ref[c, 1]
+            d_ref[c, 0] = cs_ref[n, c, 0] - res[nb:half]
 
     def columns(c):
         return pl.ds(c * CHUNK, CHUNK)
@@ -391,53 +400,52 @@
             def _():
                 give(i).start()
 
-    early = d < FIRST
-
-    @pl.when(early)
-    def _():
-        give_all()
-
+    give_all()
     lead = min(LEAD // n_col, n_peers)
     soon = min(FIRST // n_col, lead)
     for j in range(soon):
         pass_on(j)
 
-    @pl.when(jnp.logical_not(early))
-    def _():
-        give_all()
-
     send_on(0)
     need(0)
     ops = prepare_even(0, 0)
+    send_on(1)
     arrive(0)
     prepare_odd(0, 0, *ops)
     eig_copy.wait()
     for c in range(n_chunks):
         x = project(e_ref[:, columns(c)], 0)
-        d_ref[c] = x
         for k in range(2):
-            cs_ref[0, c, k] = x[k * nb : (k + 1) * nb]
+            part = x[k * nb : (k + 1) * nb]
+            d_ref[c, k] = part
+            cs_ref[0, c, k] = part
             launch(k, 0, c)
 
-    for r in range(1, min(3, rounds)):
-        send_on(r)
-        need(2 * r)
+    for j in range(soon, lead):
+        pass_on(j)
     for c in range(n_chunks):
         y_ref[c] = reflect(e_ref[:, columns(c)], 0)
     for r in range(1, min(3, rounds)):
+        if r > 1:
+            send_on(r)
+        need(2 * r)
         arrive(r)
         prepare(r, r, r)
         swap_start(r)
-    for c in range(n_chunks):
-        g_ref[c] = project(y_ref[c], 1)
-    for j in range(soon, lead):
-        pass_on(j)
+        if r == 1:
+            for c in range(n_chunks):
+                x = project(y_ref[c], 1)
+                g_ref[c, 0] = x[:nb]
+                g_ref[c, 1] = x[nb:]
     for r in range(3, min(AHEAD, rounds)):
         send_on(r)
+    combine(1, 1)
 
     def step(r, carry):
         p = lax.rem(r, SLOTS)
         n = lax.rem(r + 1, SLOTS)
+        for c in range(n_chunks):
+            land(1, p, c)
         for c in range(n_chunks):
             answer(1, p, n, c)
 
@@ -452,45 +460,66 @@
         swap_start(r + 3, later)
 
         for c in range(n_chunks):
+            land(0, p, c)
             answer(0, p, n, c)
 
-        for k in range(2):
-            only(has_edge[k], lambda k=k: swap(k, r + 1).wait())
-        both, low_part = diagonal(r + 1, n)
         for c in range(n_chunks):
-            y_ref[c] = reflect(corrected(p, c), n)
+            y_ref[c] = reflect(y_ref[c], n)
+        q = lax.rem(r + 2, SLOTS)
         for c in range(n_chunks):
-            g_ref[c] = project(y_ref[c], lax.rem(r + 2, SLOTS))
+            x = project(y_ref[c], q)
+            g_ref[c, 0] = x[:nb]
+            g_ref[c, 1] = x[nb:]
+        combine(jnp.minimum(r + 2, rounds - 1), q, r + 2 < rounds)
+        return carry
+
+    lax.fori_loop(0, rounds - 1, step, 0)
+
+    p = (rounds - 1) % SLOTS
+    for k in (1, 0):
         for c in range(n_chunks):
-            less = dot(both, st_ref[c]) + dot(low_part, st_ref[c, pl.ds(0, half)])
-            for k in range(2):
-                d_ref[c, pl.ds(k * nb, nb)] = cs_ref[n, c, k] - less[k * nb : (k + 1) * nb]
-        return carry
-
-    lax.fori_loop(0, rounds - 1, step, 0)
-
-    p = (rounds - 1) % SLOTS
-    for c in range(n_chunks):
-        for k in (1, 0):
             land(k, p, c)
-            total(k, p, c)
-        out_ref[:, columns(c)] = corrected(p, c)
-
-    for j in range(n_peers):
-
-        @pl.when(peer(j) != d)
-        def _():
-            give(j).wait_send()
-            for o in range(1, n_col):
-                relay(j, o).wait_send()
+            out_ref[side(k), columns(c)] = y_ref[c, side(k)] - dot(
+                op_ref[p, k, pl.ds(half, half)], total(k, p, c)
+            )
+
+    def sent(sem, src, dst):
+        pltpu.make_async_remote_copy(
+            src_ref=src,
+            dst_ref=dst,
+            send_sem=sem,
+            recv_sem=frecv_sem.at[0],
+            device_id={"row": d},
+            device_id_type=MESH,
+        ).wait_send()
+
+    def gone(count):
+        blocks = pl.ds(0, count)
+        sent(asend_sem, pk_ref.at[blocks], got_ref.at[blocks])
+        if n_col > 1:
+            blocks = pl.ds(0, count * (n_col - 1))
+            sent(rsend_sem, got_ref.at[blocks], got_ref.at[blocks])
+
+    @pl.when(others > 0)
+    def _():
+        gone(n_peers)
+
+    @pl.when(others == 0)
+    def _():
+        gone(n_peers - 1)
 
     @pl.when(has_dn)
     def _():
-        def done(r, carry):
-            forward(r).wait_send()
-            return carry
-
-        lax.fori_loop(0, rounds, done, 0)
+        sent(fsend_sem, got_ref.at[pl.ds(0, rounds)], fw_ref)
+
+    for k in range(2):
+        blocks = pl.ds(0, rounds - 1)
+        only(
+            has_edge[k],
+            lambda k=k: sent(
+                hsend_sem.at[k], hsend_ref.at[blocks, k], hrecv_ref.at[blocks, k]
+            ),
+        )
 
 
 def sweep(eigvecs, reflectors, factors, first_block, n_row, n_col):
@@ -501,6 +530,8 @@
     rounds = windows // 2
     n_chunks = MAX_LIVE // CHUNK
     n_peers = n_row // n_col
+    reflectors = reflectors.reshape(n_peers, n_col, nb, band)
+    factors = factors.reshape(n_peers, n_col, nb, nb)
     vmem = pltpu.VMEM
     dma = pltpu.SemaphoreType.DMA
     hbm = pl.BlockSpec(memory_space=pltpu.HBM)
@@ -517,9 +548,8 @@
             vmem((windows, nb, block_rows), F32),
             vmem((rounds, nb, block_rows), F32),
             vmem((n_chunks, rows, CHUNK), F32),
-            vmem((n_chunks, 2 * nb, CHUNK), F32),
-            vmem((n_chunks, 2 * nb, CHUNK), F32),
-            vmem((n_chunks, 4 * nb, CHUNK), BF16),
+            vmem((n_chunks, 2, nb, CHUNK), F32),
+            vmem((n_chunks, 2, nb, CHUNK), F32),
             vmem((SLOTS, n_chunks, 2, nb, CHUNK), F32),
             vmem((SLOTS, n_chunks, 2, nb, CHUNK), F32),
             vmem((rounds + 3, 2, nb // 2, 2 * nb), F32),
@@ -528,23 +558,25 @@
             vmem((SLOTS, rows, rows), BF16),
             vmem((SLOTS, 2 * nb, rows), BF16),
             vmem((SLOTS, 2 * nb, rows), BF16),
-            vmem((SLOTS, 2, nb, 4 * nb), BF16),
-            vmem((SLOTS, 2 * nb, 2 * nb), F32),
-            vmem((SLOTS, rows, 4 * nb), BF16),
-            vmem((SLOTS, rows, 2 * nb), BF16),
-            dma((2, n_peers + 1)),
+            vmem((SLOTS, 2, nb, 2 * nb), F32),
+            vmem((SLOTS, 2, rows // 2, 2 * nb), BF16),
+            vmem((SLOTS, 2, rows // 2, 2 * nb), BF16),
+            vmem((SLOTS, 2, rows, 4 * nb), BF16),
+            dma((4,)),
             dma,
-            dma((n_peers,)),
-            dma((max(n_col - 1, 1), n_peers)),
+            dma,
+            dma,
             dma((windows,)),
             dma((2, SLOTS, n_chunks)),
             dma((2, SLOTS, n_chunks)),
-            dma((rounds,)),
-            dma((rounds,)),
-            dma((2, rounds)),
-            dma((2, rounds)),
+            dma,
+            dma((RING,)),
+            dma((2,)),
+            dma((2, RING)),
         ],
-        compiler_params=pltpu.CompilerParams(collective_id=0, has_side_effects=True),
+        compiler_params=pltpu.CompilerParams(
+            collective_id=0, has_side_effects=True, vmem_limit_bytes=53 * 2**20
+        ),
         name="sweep",
     )(first_block, eigvecs, reflectors, factors)
 

time: 99.1 us -> 94.4 us (0.953)
  Pallas kernels: 95.1 us -> 91.6 us
  other arithmetic: 2.23 us -> 1.11 us
    pallas_call x1, Pallas kernels: 95.1 us -> 91.6 us  [sweep(): pl.pallas_call(functools.partial(kernel, n_row, n_col), out_shape=jax.Sha...]
    select_n x1, other arithmetic: 2.23 us -> 1.1 us  [body(): return jnp.where(kept_mask[None, :], vectors, 0.0)]
where the time goes in v4:
time: 94.4 us; the launch traced here: 94 us
  Pallas kernels  91.6 us (97%)
  other arithmetic  1.11 us (1%)
    pallas_call x1, Pallas kernels, sweep(): pl.pallas_call(functools.partial(kernel, n_row, n_col), out_shape=jax.Sha...  91.6 us

profile of v4, /device:TPU:6, one launch (start us, length us, event | category | flops | bytes accessed | tf_op | source)
XLA Modules:
  0.0 94.0 jit_solution(3119327814145854269)
XLA Ops:
  0.7 0.0 copy-start
  0.7 0.6 copy-done
  1.3 91.6 %sweep.1 = f32[256,768]{1,0:T(8,128)S(1)} custom-call(s32[32]{0:T(128)S(1)} %copy-done, f32[256,1024]{1,0:T(8,128)} %eig_hbm.1, f32[8,4,64,192]{3,2,1,0:T(8,128)} %bitcast.4, f32[8,4,64,64]{3,2,1,0:T(8,128)} %bitcast.5), custom_call_target="tpu_custom_call" | custom-call | tf_op jit(solution)/shard_map/sweep/pallas_call | solution.py:538
  92.9 1.1 %pad_select_fusion = f32[256,1024]{1,0:T(8,128)} fusion(f32[256,768]{1,0:T(8,128)S(1)} %sweep.1, pred[1024]{0:T(1024)(128)(4,1)S(1)} %iota_compare_fusion), kind=kLoop, calls=%fused_computation | loop fusion | flops 262144 | bytes 1836032 | tf_op jit(solution)/shard_map/jit(_where)/select_n | solution.py:591
  (1 shorter events, 0.0 us)
Async XLA Ops:
  0.7 0.7 copy-start

commit v5 on v4

--- a/solution.py
+++ b/solution.py
@@ -400,10 +400,21 @@
             def _():
                 give(i).start()
 
-    give_all()
+    early = d < FIRST
+
+    @pl.when(early)
+    def _():
+        give_all()
+
     lead = min(LEAD // n_col, n_peers)
     soon = min(FIRST // n_col, lead)
-    for j in range(soon):
+    pass_on(0)
+
+    @pl.when(jnp.logical_not(early))
+    def _():
+        give_all()
+
+    for j in range(1, soon):
         pass_on(j)
 
     send_on(0)
@@ -421,13 +432,13 @@
             cs_ref[0, c, k] = part
             launch(k, 0, c)
 
+    for r in range(2, min(AHEAD, rounds)):
+        send_on(r)
     for j in range(soon, lead):
         pass_on(j)
     for c in range(n_chunks):
         y_ref[c] = reflect(e_ref[:, columns(c)], 0)
     for r in range(1, min(3, rounds)):
-        if r > 1:
-            send_on(r)
         need(2 * r)
         arrive(r)
         prepare(r, r, r)
@@ -437,8 +448,6 @@
                 x = project(y_ref[c], 1)
                 g_ref[c, 0] = x[:nb]
                 g_ref[c, 1] = x[nb:]
-    for r in range(3, min(AHEAD, rounds)):
-        send_on(r)
     combine(1, 1)
 
     def step(r, carry):

time: 94.4 us -> 93.1 us (0.986)
  Pallas kernels: 91.6 us -> 90.3 us
    pallas_call x1, Pallas kernels: 91.6 us -> 90.3 us  [sweep(): pl.pallas_call(functools.partial(kernel, n_row, n_col), out_shape=jax.Sha...]
where the time goes in v5:
time: 93.1 us; the launch traced here: 92.7 us
  Pallas kernels  90.3 us (97%)
  other arithmetic  1.11 us (1%)
    pallas_call x1, Pallas kernels, sweep(): pl.pallas_call(functools.partial(kernel, n_row, n_col), out_shape=jax.Sha...  90.3 us

profile of v5, /device:TPU:6, one launch (start us, length us, event | category | flops | bytes accessed | tf_op | source)
XLA Modules:
  0.0 92.7 jit_solution(13894051319991572208)
XLA Ops:
  0.7 0.0 copy-start
  0.7 0.6 copy-done
  1.3 90.3 %sweep.1 = f32[256,768]{1,0:T(8,128)S(1)} custom-call(s32[32]{0:T(128)S(1)} %copy-done, f32[256,1024]{1,0:T(8,128)} %eig_hbm.1, f32[8,4,64,192]{3,2,1,0:T(8,128)} %bitcast.4, f32[8,4,64,64]{3,2,1,0:T(8,128)} %bitcast.5), custom_call_target="tpu_custom_call" | custom-call | tf_op jit(solution)/shard_map/sweep/pallas_call | solution.py:547
  91.6 1.1 %pad_select_fusion = f32[256,1024]{1,0:T(8,128)} fusion(f32[256,768]{1,0:T(8,128)S(1)} %sweep.1, pred[1024]{0:T(1024)(128)(4,1)S(1)} %iota_compare_fusion), kind=kLoop, calls=%fused_computation | loop fusion | flops 262144 | bytes 1836032 | tf_op jit(solution)/shard_map/jit(_where)/select_n | solution.py:600
  (1 shorter events, 0.0 us)
Async XLA Ops:
  0.7 0.7 copy-start
